TPU v7x, 512 devices: a whole 4x8x8 slice. The times are simulated.
512 devices in a mesh: cell: 64 (over x, z, core), grp: 8 (over y).
Axes of the slice: x: 4, y: 8, z: 8, core: 2. Of those that a mesh axis runs over, the one named last changes fastest.
Arguments:
- atom_sites: float32 [3, 262144], P(None, ('cell', 'grp')), may hold values from 0 to 64, as said below
- grid_points: float32 [3, 196608], P(None, ('cell', 'grp')), may hold values from 0 to 64, as said below
- dipole_guess: float32 [3, 262144], P(None, ('cell', 'grp')), may hold values from -2 to 2
- fixed_field: float32 [3, 262144], P(None, ('cell', 'grp')), may hold values from -1800 to 1800
- polarisability: float32 [262144], P(('cell', 'grp')), may hold values from 0.0005 to 0.002
- base_charge: float32 [196608], P(('cell', 'grp')), may hold values from -12 to 12
- response: float32 [196608], P(('cell', 'grp')), may hold values from 0.02 to 0.2
- near_blocks: int32 [2048, 8], P(('cell', 'grp')), may hold values from 0 to 95, as said below
- grid_blocks: int32 [2048, 4], P(('cell', 'grp')), may hold values from 0 to 71, as said below
- source_blocks: int32 [1536, 8], P(('cell', 'grp')), may hold values from 0 to 95, as said below
Outputs:
- dipoles: float32 [3, 262144], P(None, ('cell', 'grp'))
- qm_charges: float32 [196608], P(('cell', 'grp'))
Inputs may be any that keep to these rules, and one draw needn't show every extreme that they name: `atom_sites`: atom a has first coordinate in [c, c + 1) with c = a // 4096, the other two in [0, 1). `grid_points`: grid point g has first coordinate in [c, c + 1) with c = g // 3072, the other two in [0, 1). `near_blocks`: each row holds 8 distinct MM window indices, never the block's own index 32 + b % 32. `grid_blocks`: each row holds 4 distinct grid window indices. `source_blocks`: each row holds 8 distinct MM window indices.
All inputs are finite; a program needn't handle non-finite values.
Results may differ from a plain program's by a relative error of at most 0.0003.
Values sent between devices are 32-bit elements; how exact they have to be, the bound alone decides.
A program may use at most 64 MiB of HBM per device.

v0:
```python
import jax
import jax.numpy as jnp
from jax import lax
from jax.sharding import PartitionSpec as P

BLOCK = 128
ITERS = 3


soften_sq = 0.04


def laid_out(pieces, dim):
    pieces = jnp.moveaxis(pieces, 0, dim)
    lengths = pieces.shape
    return pieces.reshape(*lengths[:dim], lengths[dim] * lengths[dim + 1], *lengths[dim + 2 :])


def copy_for_each(x, axis):
    copies = jnp.broadcast_to(x, (lax.axis_size(axis), *x.shape))
    return lax.all_to_all(copies, axis, split_axis=0, concat_axis=0, tiled=True)


def gather_directly(x, axis, dim):
    return laid_out(copy_for_each(x, axis), dim)


def with_halo(x, sides, width):
    for axis, dim in sides:
        peers, length = (lax.axis_size(axis), x.shape[dim])
        up = [(i, (i + 1) % peers) for i in range(peers - 1)]
        down = [(j, i) for i, j in up]
        last = lax.slice_in_dim(x, length - width, length, axis=dim)
        initial = lax.slice_in_dim(x, 0, width, axis=dim)
        before = lax.ppermute(last, axis, up)
        after = lax.ppermute(initial, axis, down)
        x = jnp.concatenate([before, x, after], axis=dim)
    return x


def taken_together(x, axis):
    everything = copy_for_each(x, axis)
    return jnp.sum(everything, axis=0)


def pair_geometry(targets, sources):
    delta_x = targets[0][:, None] - sources[0][None, :]
    delta_y = targets[1][:, None] - sources[1][None, :]
    delta_z = targets[2][:, None] - sources[2][None, :]
    inverse = 1.0 / jnp.sqrt(delta_x * delta_x + delta_y * delta_y + delta_z * delta_z + soften_sq)
    inv_cube = inverse * inverse * inverse
    return (delta_x, delta_y, delta_z, inv_cube, inv_cube * inverse * inverse)


def dipole_field(targets, sources, moments, keep_mask):
    delta_x, delta_y, delta_z, inv_cube, inv_fifth = pair_geometry(targets, sources)
    projected = (
        moments[0][None, :] * delta_x
        + moments[1][None, :] * delta_y
        + moments[2][None, :] * delta_z
    )
    radial = 3.0 * projected * inv_fifth * keep_mask
    direct = inv_cube * keep_mask
    return jnp.stack(
        [
            jnp.sum(radial * delta_x - moments[0][None, :] * direct, axis=1),
            jnp.sum(radial * delta_y - moments[1][None, :] * direct, axis=1),
            jnp.sum(radial * delta_z - moments[2][None, :] * direct, axis=1),
        ]
    )


def charge_field(targets, sources, charges):
    delta_x, delta_y, delta_z, inv_cube, inv_fifth = pair_geometry(targets, sources)
    weight = charges[None, :] * inv_cube
    return jnp.stack(
        [
            jnp.sum(weight * delta_x, axis=1),
            jnp.sum(weight * delta_y, axis=1),
            jnp.sum(weight * delta_z, axis=1),
        ]
    )


def dipole_potential(targets, sources, moments):
    delta_x, delta_y, delta_z, inv_cube, inv_fifth = pair_geometry(targets, sources)
    projected = (
        moments[0][None, :] * delta_x
        + moments[1][None, :] * delta_y
        + moments[2][None, :] * delta_z
    )
    return jnp.sum(projected * inv_cube, axis=1)


def far_geometry(targets, cell_here, cell_count):
    centres = jnp.arange(cell_count, dtype=jnp.int32).astype(jnp.float32) + 0.5
    delta_x = targets[0][None, :] - centres[:, None]
    delta_y = targets[1][None, :] - 0.5
    delta_z = targets[2][None, :] - 0.5
    far_mask = (jnp.abs(jnp.arange(cell_count, dtype=jnp.int32) - cell_here) >= 2).astype(
        jnp.float32
    )[:, None]
    inverse = 1.0 / jnp.sqrt(delta_x * delta_x + delta_y * delta_y + delta_z * delta_z + soften_sq)
    inv_cube = inverse * inverse * inverse * far_mask
    return (delta_x, delta_y, delta_z, inv_cube, inv_cube * inverse * inverse)


def far_field(targets, cell_here, moments, charges):
    delta_x, delta_y, delta_z, inv_cube, inv_fifth = far_geometry(
        targets, cell_here, charges.shape[0]
    )
    projected = moments[:, 0:1] * delta_x + moments[:, 1:2] * delta_y + moments[:, 2:3] * delta_z
    radial = 3.0 * projected * inv_fifth
    coulomb = charges[:, None] * inv_cube
    return jnp.stack(
        [
            jnp.sum(radial * delta_x - moments[:, 0:1] * inv_cube + coulomb * delta_x, axis=0),
            jnp.sum(radial * delta_y - moments[:, 1:2] * inv_cube + coulomb * delta_y, axis=0),
            jnp.sum(radial * delta_z - moments[:, 2:3] * inv_cube + coulomb * delta_z, axis=0),
        ]
    )


def far_potential(targets, cell_here, moments):
    delta_x, delta_y, delta_z, inv_cube, inv_fifth = far_geometry(
        targets, cell_here, moments.shape[0]
    )
    projected = moments[:, 0:1] * delta_x + moments[:, 1:2] * delta_y + moments[:, 2:3] * delta_z
    return jnp.sum(projected * inv_cube, axis=0)


def listed_tiles(tile_set, index_lists):
    taken = jnp.take(tile_set, index_lists, axis=1)
    count, listed = index_lists.shape
    return jnp.transpose(taken, (1, 0, 2, 3)).reshape(count, 3, listed * tile_set.shape[2])


def spread(payload):
    lifted = payload[:, None, None, :]
    members = gather_directly(lifted, "grp", 2)
    return with_halo(members, (("cell", 1),), 1)


def body(
    atom_sites,
    grid_points,
    dipole_guess,
    fixed_field,
    polarisability,
    base_charge,
    response,
    near_blocks,
    grid_blocks,
    source_blocks,
):
    groups = lax.axis_size("grp")
    cell_here = lax.axis_index("cell")
    grp_here = lax.axis_index("grp")
    local_blocks = near_blocks.shape[0]
    local_gblocks = source_blocks.shape[0]
    atom_count = atom_sites.shape[1]
    grid_count = grid_points.shape[1]
    cell_blocks = local_blocks * groups
    cell_gblocks = local_gblocks * groups
    statics = spread(jnp.concatenate([atom_sites, grid_points], axis=1))
    site_tiles = statics[:, :, :, :atom_count].reshape(3, 3 * cell_blocks, BLOCK)
    point_tiles = statics[:, :, :, atom_count:].reshape(3, 3 * cell_gblocks, BLOCK)
    atom_targets = jnp.transpose(atom_sites.reshape(3, local_blocks, BLOCK), (1, 0, 2))
    grid_targets = jnp.transpose(grid_points.reshape(3, local_gblocks, BLOCK), (1, 0, 2))
    own_slots = cell_blocks + grp_here * local_blocks + jnp.arange(local_blocks, dtype=jnp.int32)
    atom_lists = jnp.concatenate([own_slots[:, None], near_blocks], axis=1)
    near_sites = listed_tiles(site_tiles, atom_lists)
    grid_sites = listed_tiles(point_tiles, grid_blocks)
    source_sites = listed_tiles(site_tiles, source_blocks)
    keep_mask = jnp.concatenate(
        [
            1.0 - jnp.eye(BLOCK, dtype=jnp.float32),
            jnp.ones((BLOCK, near_blocks.shape[1] * BLOCK), jnp.float32),
        ],
        axis=1,
    )
    centre = jnp.stack(
        [
            cell_here.astype(jnp.float32) + 0.5,
            jnp.array(0.5, jnp.float32),
            jnp.array(0.5, jnp.float32),
        ]
    )
    offsets = grid_points - centre[:, None]
    dipoles = dipole_guess
    charges = base_charge
    for iteration in range(ITERS):
        shared = spread(jnp.concatenate([dipoles, charges.reshape(3, grid_count // 3)], axis=1))
        dipole_tiles = shared[:, :, :, :atom_count].reshape(3, 3 * cell_blocks, BLOCK)
        charge_tiles = jnp.transpose(shared[:, :, :, atom_count:], (1, 2, 0, 3)).reshape(
            3 * cell_gblocks, BLOCK
        )
        local_sums = jnp.concatenate(
            [
                jnp.sum(dipoles, axis=1),
                jnp.sum(charges)[None],
                jnp.sum(charges[None, :] * offsets, axis=1),
            ]
        )
        cell_sums = taken_together(local_sums, "grp")
        moment_table = gather_directly(cell_sums[None, :], "cell", 0)
        dipole_sums = moment_table[:, 0:3]
        charge_sums = moment_table[:, 3]
        moments = dipole_sums + moment_table[:, 4:7]
        near_dipoles = listed_tiles(dipole_tiles, atom_lists)
        source_dipoles = listed_tiles(dipole_tiles, source_blocks)
        grid_charges = jnp.take(charge_tiles, grid_blocks, axis=0).reshape(local_blocks, -1)

        def one_atom_block(block_args):
            targets, sources, source_moments, points, point_charges = block_args
            accumulated = dipole_field(targets, sources, source_moments, keep_mask)
            accumulated = accumulated + charge_field(targets, points, point_charges)
            return accumulated + far_field(targets, cell_here, moments, charge_sums)

        def one_grid_block(block_args):
            targets, sources, source_moments = block_args
            return dipole_potential(targets, sources, source_moments) + far_potential(
                targets, cell_here, dipole_sums
            )

        induced_field = lax.map(
            one_atom_block, (atom_targets, near_sites, near_dipoles, grid_sites, grid_charges)
        )
        induced_field = jnp.transpose(induced_field, (1, 0, 2)).reshape(3, atom_count)
        potential = lax.map(one_grid_block, (grid_targets, source_sites, source_dipoles)).reshape(
            grid_count
        )
        dipoles = polarisability[None, :] * (fixed_field + induced_field)
        charges = base_charge - response * potential
    return (dipoles, charges)


def solution(mesh):
    return jax.shard_map(
        body,
        mesh=mesh,
        in_specs=(
            P(None, ("cell", "grp")),
            P(None, ("cell", "grp")),
            P(None, ("cell", "grp")),
            P(None, ("cell", "grp")),
            P(("cell", "grp")),
            P(("cell", "grp")),
            P(("cell", "grp")),
            P(("cell", "grp"), None),
            P(("cell", "grp"), None),
            P(("cell", "grp"), None),
        ),
        out_specs=(P(None, ("cell", "grp")), P(("cell", "grp"))),
        check_vma=False,
    )
```

profile of v0, /device:TPU:1, one launch (start us, length us, event | category | flops | bytes accessed | tf_op | source)
XLA Modules:
  0.0 200.5 jit_solution(17839278385963394076)
XLA Ops:
  0.7 0.7 copy-done.2
  2.2 0.7 pad_maximum_fusion.9
  3.6 7.8 %all-to-all-start.2 = ((f32[8,1,7]{2,1,0:T(1,128)}), f32[8,1,7]{2,1,0:T(1,128)S(1)}, u32[]{:S(2)}, u32[]{:S(2)}) async-start(f32[8,1,7]{2,1,0:T(1,128)} %broadcast_in_dim.122), calls=%async_computation.2 | async-start | bytes 8192 | tf_op jit(solution)/shard_map/all_to_all | solution.py:21
  11.4 0.7 copy-done.8
  12.2 0.7 copy-done.1
  12.9 0.7 copy-done.9
  13.8 4.0 %all-to-all-done.2 = f32[8,1,7]{2,1,0:T(1,128)S(1)} async-done(((f32[8,1,7]{2,1,0:T(1,128)}), f32[8,1,7]{2,1,0:T(1,128)S(1)}, u32[]{:S(2)}, u32[]{:S(2)}) %all-to-all-start.2) | async-done | bytes 256 | tf_op jit(solution)/shard_map/all_to_all | solution.py:21
  17.8 0.7 broadcast_in_dim.116
  18.5 3.3 %all-to-all-start = ((f32[8,3,1,1,640]{4,3,2,1,0:T(1,128)}), f32[8,3,1,1,640]{4,3,2,1,0:T(1,128)S(1)}, u32[]{:S(2)}, u32[]{:S(2)}) async-start(f32[8,3,1,1,640]{4,3,2,1,0:T(1,128)} %broadcast_in_dim.116), calls=%async_computation | async-start | bytes 122880 | tf_op jit(solution)/shard_map/all_to_all | solution.py:21
  21.9 7.1 %all-to-all-done = f32[8,3,1,1,640]{4,3,2,1,0:T(1,128)S(1)} async-done(((f32[8,3,1,1,640]{4,3,2,1,0:T(1,128)}), f32[8,3,1,1,640]{4,3,2,1,0:T(1,128)S(1)}, u32[]{:S(2)}, u32[]{:S(2)}) %all-to-all-start) | async-done | bytes 61472 | tf_op jit(solution)/shard_map/all_to_all | solution.py:21
  28.9 0.6 broadcast_in_dim.123
  29.6 16.6 %all-to-all-start.3 = ((f32[64,1,7]{2,1,0:T(1,128)}), f32[64,1,7]{2,1,0:T(1,128)S(1)}, u32[]{:S(2)}, u32[]{:S(2)}) async-start(f32[64,1,7]{2,1,0:T(1,128)} %broadcast_in_dim.123), calls=%async_computation.3 | async-start | bytes 65536 | tf_op jit(solution)/shard_map/all_to_all | solution.py:21
  46.2 2.4 %collective-permute-start.1 = (f32[3,1,8,640]{3,2,0,1:T(8,128)S(1)}, f32[3,1,8,640]{3,2,0,1:T(8,128)S(1)}, u32[]{:S(2)}, u32[]{:S(2)}) collective-permute-start(f32[3,1,8,640]{3,2,0,1:T(8,128)S(1)} %bitcast.555), channel_id=1, source_target_pairs={{8,0},{16,8},{24,16},{32,24},{40,32},{48,40},{56,48},{64,56},{72,6... | collective-permute-start | bytes 184328 | tf_op jit(solution)/shard_map/ppermute | solution.py:36
  48.6 3.2 %collective-permute-start = (f32[3,1,8,640]{3,2,0,1:T(8,128)S(1)}, f32[3,1,8,640]{3,2,0,1:T(8,128)S(1)}, u32[]{:S(2)}, u32[]{:S(2)}) collective-permute-start(f32[3,1,8,640]{3,2,0,1:T(8,128)S(1)} %bitcast.556), channel_id=1, source_target_pairs={{0,8},{8,16},{16,24},{24,32},{32,40},{40,48},{48,56},{56,64},{64,7... | collective-permute-start | bytes 184328 | tf_op jit(solution)/shard_map/ppermute | solution.py:35
  51.8 3.7 %all-to-all-done.3 = f32[64,1,7]{2,1,0:T(1,128)S(1)} async-done(((f32[64,1,7]{2,1,0:T(1,128)}), f32[64,1,7]{2,1,0:T(1,128)S(1)}, u32[]{:S(2)}, u32[]{:S(2)}) %all-to-all-start.3) | async-done | bytes 1824 | tf_op jit(solution)/shard_map/all_to_all | solution.py:21
  55.5 0.7 broadcast_in_dim.117
  56.1 3.4 %all-to-all-start.1 = ((f32[8,3,1,1,896]{4,3,2,1,0:T(1,128)}), f32[8,3,1,1,896]{4,3,2,1,0:T(1,128)S(1)}, u32[]{:S(2)}, u32[]{:S(2)}) async-start(f32[8,3,1,1,896]{4,3,2,1,0:T(1,128)} %broadcast_in_dim.117), calls=%async_computation.1 | async-start | bytes 172032 | tf_op jit(solution)/shard_map/all_to_all | solution.py:21
  59.9 7.0 %all-to-all-done.1 = f32[8,3,1,1,896]{4,3,2,1,0:T(1,128)S(1)} async-done(((f32[8,3,1,1,896]{4,3,2,1,0:T(1,128)}), f32[8,3,1,1,896]{4,3,2,1,0:T(1,128)S(1)}, u32[]{:S(2)}, u32[]{:S(2)}) %all-to-all-start.1) | async-done | bytes 86048 | tf_op jit(solution)/shard_map/all_to_all | solution.py:21
  66.9 3.7 %collective-permute-start.3 = (f32[3,1,8,896]{3,2,0,1:T(8,128)S(1)}, f32[3,1,8,896]{3,2,0,1:T(8,128)S(1)}, u32[]{:S(2)}, u32[]{:S(2)}) collective-permute-start(f32[3,1,8,896]{3,2,0,1:T(8,128)S(1)} %bitcast.551), channel_id=1, source_target_pairs={{8,0},{16,8},{24,16},{32,24},{40,32},{48,40},{56,48},{64,56},{72,6... | collective-permute-start | bytes 258056 | tf_op jit(solution)/shard_map/ppermute | solution.py:36
  70.6 2.2 %collective-permute-start.2 = (f32[3,1,8,896]{3,2,0,1:T(8,128)S(1)}, f32[3,1,8,896]{3,2,0,1:T(8,128)S(1)}, u32[]{:S(2)}, u32[]{:S(2)}) collective-permute-start(f32[3,1,8,896]{3,2,0,1:T(8,128)S(1)} %bitcast.552), channel_id=1, source_target_pairs={{0,8},{8,16},{16,24},{24,32},{32,40},{40,48},{48,56},{56,64},{64,7... | collective-permute-start | bytes 258056 | tf_op jit(solution)/shard_map/ppermute | solution.py:35
  74.3 0.6 gather_fusion.1
  75.7 0.6 gather_fusion.2
  77.3 2.5 %while.79 = (s32[]{:T(128)}, f32[3,128]{1,0:T(4,128)S(1)}, f32[3,3,1024]{2,0,1:T(4,128)S(1)}, f32[3,3,128]{2,1,0:T(4,128)S(1)}, f32[3,3,1024]{2,1,0:T(4,128)S(1)...) while((s32[]{:T(128)}, f32[3,128]{1,0:T(4,128)S(1)}, ...), condition=%wide.region_18.22_spmd, body=%wide.region_15.21_spmd.sunk | while | flops 2482948 | bytes 94129 | solution.py:230
  80.8 6.5 %while.78 = (s32[]{:T(128)}, f32[4,3,128]{2,1,0:T(4,128)S(1)}, f32[4,3,1152]{2,1,0:T(4,128)S(1)}, f32[4,3,128]{2,1,0:T(4,128)S(1)}, f32[4,3,1152]{2,1,0:T(4,128)...) while((s32[]{:T(128)}, f32[4,3,128]{2,1,0:T(4,128)S(1)}, ...), condition=%wide.region_14.17_spmd, body=%wide.region_4.16_spmd.sunk | while | flops 6490884 | bytes 727253 | solution.py:226
  81.5 0.9 fusion.208
  83.1 0.9 fusion.208
  84.7 0.9 fusion.208
  86.4 0.9 fusion.208
  87.4 0.7 pad_maximum_fusion.10
  88.7 3.3 %all-to-all-start.5 = ((f32[8,1,7]{2,1,0:T(1,128)}), f32[8,1,7]{2,1,0:T(1,128)S(1)}, u32[]{:S(2)}, u32[]{:S(2)}) async-start(f32[8,1,7]{2,1,0:T(1,128)} %broadcast_in_dim.126), calls=%async_computation.5 | async-start | bytes 8192 | tf_op jit(solution)/shard_map/all_to_all | solution.py:21
  92.1 6.4 %all-to-all-done.5 = f32[8,1,7]{2,1,0:T(1,128)S(1)} async-done(((f32[8,1,7]{2,1,0:T(1,128)}), f32[8,1,7]{2,1,0:T(1,128)S(1)}, u32[]{:S(2)}, u32[]{:S(2)}) %all-to-all-start.5) | async-done | bytes 256 | tf_op jit(solution)/shard_map/all_to_all | solution.py:21
  98.5 0.7 broadcast_in_dim.124
  99.1 3.3 %all-to-all-start.4 = ((f32[8,3,1,1,640]{4,3,2,1,0:T(1,128)}), f32[8,3,1,1,640]{4,3,2,1,0:T(1,128)S(1)}, u32[]{:S(2)}, u32[]{:S(2)}) async-start(f32[8,3,1,1,640]{4,3,2,1,0:T(1,128)} %broadcast_in_dim.124), calls=%async_computation.4 | async-start | bytes 122880 | tf_op jit(solution)/shard_map/all_to_all | solution.py:21
  102.5 7.1 %all-to-all-done.4 = f32[8,3,1,1,640]{4,3,2,1,0:T(1,128)S(1)} async-done(((f32[8,3,1,1,640]{4,3,2,1,0:T(1,128)}), f32[8,3,1,1,640]{4,3,2,1,0:T(1,128)S(1)}, u32[]{:S(2)}, u32[]{:S(2)}) %all-to-all-start.4) | async-done | bytes 61472 | tf_op jit(solution)/shard_map/all_to_all | solution.py:21
  109.6 0.6 broadcast_in_dim.127
  110.2 11.4 %all-to-all-start.6 = ((f32[64,1,7]{2,1,0:T(1,128)}), f32[64,1,7]{2,1,0:T(1,128)S(1)}, u32[]{:S(2)}, u32[]{:S(2)}) async-start(f32[64,1,7]{2,1,0:T(1,128)} %broadcast_in_dim.127), calls=%async_computation.6 | async-start | bytes 65536 | tf_op jit(solution)/shard_map/all_to_all | solution.py:21
  121.6 2.4 %collective-permute-start.5 = (f32[3,1,8,640]{3,2,0,1:T(8,128)S(1)}, f32[3,1,8,640]{3,2,0,1:T(8,128)S(1)}, u32[]{:S(2)}, u32[]{:S(2)}) collective-permute-start(f32[3,1,8,640]{3,2,0,1:T(8,128)S(1)} %bitcast.563), channel_id=1, source_target_pairs={{8,0},{16,8},{24,16},{32,24},{40,32},{48,40},{56,48},{64,56},{72,6... | collective-permute-start | bytes 184328 | tf_op jit(solution)/shard_map/ppermute | solution.py:36
  124.0 3.2 %collective-permute-start.4 = (f32[3,1,8,640]{3,2,0,1:T(8,128)S(1)}, f32[3,1,8,640]{3,2,0,1:T(8,128)S(1)}, u32[]{:S(2)}, u32[]{:S(2)}) collective-permute-start(f32[3,1,8,640]{3,2,0,1:T(8,128)S(1)} %bitcast.564), channel_id=1, source_target_pairs={{0,8},{8,16},{16,24},{24,32},{32,40},{40,48},{48,56},{56,64},{64,7... | collective-permute-start | bytes 184328 | tf_op jit(solution)/shard_map/ppermute | solution.py:35
  127.2 3.7 %all-to-all-done.6 = f32[64,1,7]{2,1,0:T(1,128)S(1)} async-done(((f32[64,1,7]{2,1,0:T(1,128)}), f32[64,1,7]{2,1,0:T(1,128)S(1)}, u32[]{:S(2)}, u32[]{:S(2)}) %all-to-all-start.6) | async-done | bytes 1824 | tf_op jit(solution)/shard_map/all_to_all | solution.py:21
  132.1 0.6 gather_fusion.6
  133.6 6.5 %while.80 = (s32[]{:T(128)}, f32[4,3,128]{2,1,0:T(4,128)S(1)}, f32[4,3,1152]{2,1,0:T(4,128)S(1)}, f32[4,3,128]{2,1,0:T(4,128)S(1)}, f32[4,3,1152]{2,1,0:T(4,128)...) while((s32[]{:T(128)}, f32[4,3,128]{2,1,0:T(4,128)S(1)}, ...), condition=%wide.region_33.37_spmd, body=%wide.region_23.36_spmd.sunk | while | flops 6490884 | bytes 727253 | solution.py:226
  134.3 0.9 fusion.213
  135.9 0.9 fusion.213
  137.6 0.9 fusion.213
  139.2 0.9 fusion.213
  140.3 2.5 %while.81 = (s32[]{:T(128)}, f32[3,128]{1,0:T(4,128)S(1)}, f32[3,3,1024]{2,0,1:T(4,128)S(1)}, f32[3,3,128]{2,1,0:T(4,128)S(1)}, f32[3,3,1024]{2,1,0:T(4,128)S(1)...) while((s32[]{:T(128)}, f32[3,128]{1,0:T(4,128)S(1)}, ...), condition=%wide.region_37.41_spmd, body=%wide.region_34.40_spmd.sunk | while | flops 2482948 | bytes 94129 | solution.py:230
  143.6 0.7 pad_maximum_fusion.11
  144.9 3.3 %all-to-all-start.8 = ((f32[8,1,7]{2,1,0:T(1,128)}), f32[8,1,7]{2,1,0:T(1,128)S(1)}, u32[]{:S(2)}, u32[]{:S(2)}) async-start(f32[8,1,7]{2,1,0:T(1,128)} %broadcast_in_dim.130), calls=%async_computation.8 | async-start | bytes 8192 | tf_op jit(solution)/shard_map/all_to_all | solution.py:21
  148.2 6.4 %all-to-all-done.8 = f32[8,1,7]{2,1,0:T(1,128)S(1)} async-done(((f32[8,1,7]{2,1,0:T(1,128)}), f32[8,1,7]{2,1,0:T(1,128)S(1)}, u32[]{:S(2)}, u32[]{:S(2)}) %all-to-all-start.8) | async-done | bytes 256 | tf_op jit(solution)/shard_map/all_to_all | solution.py:21
  154.6 0.7 broadcast_in_dim.128
  155.3 3.3 %all-to-all-start.7 = ((f32[8,3,1,1,640]{4,3,2,1,0:T(1,128)}), f32[8,3,1,1,640]{4,3,2,1,0:T(1,128)S(1)}, u32[]{:S(2)}, u32[]{:S(2)}) async-start(f32[8,3,1,1,640]{4,3,2,1,0:T(1,128)} %broadcast_in_dim.128), calls=%async_computation.7 | async-start | bytes 122880 | tf_op jit(solution)/shard_map/all_to_all | solution.py:21
  158.7 7.2 %all-to-all-done.7 = f32[8,3,1,1,640]{4,3,2,1,0:T(1,128)S(1)} async-done(((f32[8,3,1,1,640]{4,3,2,1,0:T(1,128)}), f32[8,3,1,1,640]{4,3,2,1,0:T(1,128)S(1)}, u32[]{:S(2)}, u32[]{:S(2)}) %all-to-all-start.7) | async-done | bytes 61472 | tf_op jit(solution)/shard_map/all_to_all | solution.py:21
  165.8 0.6 broadcast_in_dim.131
  166.4 11.8 %all-to-all-start.9 = ((f32[64,1,7]{2,1,0:T(1,128)}), f32[64,1,7]{2,1,0:T(1,128)S(1)}, u32[]{:S(2)}, u32[]{:S(2)}) async-start(f32[64,1,7]{2,1,0:T(1,128)} %broadcast_in_dim.131), calls=%async_computation.9 | async-start | bytes 65536 | tf_op jit(solution)/shard_map/all_to_all | solution.py:21
  178.2 2.4 %collective-permute-start.7 = (f32[3,1,8,640]{3,2,0,1:T(8,128)S(1)}, f32[3,1,8,640]{3,2,0,1:T(8,128)S(1)}, u32[]{:S(2)}, u32[]{:S(2)}) collective-permute-start(f32[3,1,8,640]{3,2,0,1:T(8,128)S(1)} %bitcast.559), channel_id=1, source_target_pairs={{8,0},{16,8},{24,16},{32,24},{40,32},{48,40},{56,48},{64,56},{72,6... | collective-permute-start | bytes 184328 | tf_op jit(solution)/shard_map/ppermute | solution.py:36
  180.6 3.4 %collective-permute-start.6 = (f32[3,1,8,640]{3,2,0,1:T(8,128)S(1)}, f32[3,1,8,640]{3,2,0,1:T(8,128)S(1)}, u32[]{:S(2)}, u32[]{:S(2)}) collective-permute-start(f32[3,1,8,640]{3,2,0,1:T(8,128)S(1)} %bitcast.560), channel_id=1, source_target_pairs={{0,8},{8,16},{16,24},{24,32},{32,40},{40,48},{48,56},{56,64},{64,7... | collective-permute-start | bytes 184328 | tf_op jit(solution)/shard_map/ppermute | solution.py:35
  184.0 3.5 %all-to-all-done.9 = f32[64,1,7]{2,1,0:T(1,128)S(1)} async-done(((f32[64,1,7]{2,1,0:T(1,128)}), f32[64,1,7]{2,1,0:T(1,128)S(1)}, u32[]{:S(2)}, u32[]{:S(2)}) %all-to-all-start.9) | async-done | bytes 1824 | tf_op jit(solution)/shard_map/all_to_all | solution.py:21
  188.7 0.6 gather_fusion.9
  190.2 6.5 %while.82 = (s32[]{:T(128)}, f32[4,3,128]{2,1,0:T(4,128)S(1)}, f32[4,3,1152]{2,1,0:T(4,128)S(1)}, f32[4,3,128]{2,1,0:T(4,128)S(1)}, f32[4,3,1152]{2,1,0:T(4,128)...) while((s32[]{:T(128)}, f32[4,3,128]{2,1,0:T(4,128)S(1)}, ...), condition=%wide.region_52.56_spmd, body=%wide.region_42.55_spmd.sunk | while | flops 6490884 | bytes 727253 | solution.py:226
  190.9 0.9 fusion.218
  192.6 0.9 fusion.218
  194.2 0.9 fusion.218
  195.8 0.9 fusion.218
  197.4 2.5 %while.83 = (s32[]{:T(128)}, f32[3,128]{1,0:T(4,128)S(1)}, f32[3,3,1024]{2,0,1:T(4,128)S(1)}, f32[3,3,128]{2,1,0:T(4,128)S(1)}, f32[3,3,1024]{2,1,0:T(4,128)S(1)...) while((s32[]{:T(128)}, f32[3,128]{1,0:T(4,128)S(1)}, ...), condition=%wide.region_56.60_spmd, body=%wide.region_53.59_spmd.sunk | while | flops 2482948 | bytes 94129 | solution.py:230
  (399 shorter events, 28.6 us)
Async XLA Ops:
  0.6 1.3 copy-start.4
  0.6 0.7 copy-start.2
  1.3 0.7 copy-start
  3.6 7.8 %copy-start.7 = (s32[4,4]{1,0:T(4,128)S(1)}, s32[4,4]{1,0:T(4,128)}, u32[]{:S(2)}) copy-start(s32[4,4]{1,0:T(4,128)} %param.36) | copy-start | bytes 196
  3.6 14.3 %all-to-all-start.2 = ((f32[8,1,7]{2,1,0:T(1,128)}), f32[8,1,7]{2,1,0:T(1,128)S(1)}, u32[]{:S(2)}, u32[]{:S(2)}) async-start(f32[8,1,7]{2,1,0:T(1,128)} %broadcast_in_dim.122), calls=%async_computation.2 | async-start | bytes 8192 | tf_op jit(solution)/shard_map/all_to_all | solution.py:21
  11.4 0.7 copy-start.8
  12.2 0.7 copy-start.1
  12.9 0.7 copy-start.9
  18.5 10.5 %all-to-all-start = ((f32[8,3,1,1,640]{4,3,2,1,0:T(1,128)}), f32[8,3,1,1,640]{4,3,2,1,0:T(1,128)S(1)}, u32[]{:S(2)}, u32[]{:S(2)}) async-start(f32[8,3,1,1,640]{4,3,2,1,0:T(1,128)} %broadcast_in_dim.116), calls=%async_computation | async-start | bytes 122880 | tf_op jit(solution)/shard_map/all_to_all | solution.py:21
  29.6 25.9 %all-to-all-start.3 = ((f32[64,1,7]{2,1,0:T(1,128)}), f32[64,1,7]{2,1,0:T(1,128)S(1)}, u32[]{:S(2)}, u32[]{:S(2)}) async-start(f32[64,1,7]{2,1,0:T(1,128)} %broadcast_in_dim.123), calls=%async_computation.3 | async-start | bytes 65536 | tf_op jit(solution)/shard_map/all_to_all | solution.py:21
  46.2 26.5 %collective-permute-start.1 = (f32[3,1,8,640]{3,2,0,1:T(8,128)S(1)}, f32[3,1,8,640]{3,2,0,1:T(8,128)S(1)}, u32[]{:S(2)}, u32[]{:S(2)}) collective-permute-start(f32[3,1,8,640]{3,2,0,1:T(8,128)S(1)} %bitcast.555), channel_id=1, source_target_pairs={{8,0},{16,8},{24,16},{32,24},{40,32},{48,40},{56,48},{64,56},{72,6... | collective-permute-start | bytes 184328 | tf_op jit(solution)/shard_map/ppermute | solution.py:36
  48.6 24.2 %collective-permute-start = (f32[3,1,8,640]{3,2,0,1:T(8,128)S(1)}, f32[3,1,8,640]{3,2,0,1:T(8,128)S(1)}, u32[]{:S(2)}, u32[]{:S(2)}) collective-permute-start(f32[3,1,8,640]{3,2,0,1:T(8,128)S(1)} %bitcast.556), channel_id=1, source_target_pairs={{0,8},{8,16},{16,24},{24,32},{32,40},{40,48},{48,56},{56,64},{64,7... | collective-permute-start | bytes 184328 | tf_op jit(solution)/shard_map/ppermute | solution.py:35
  56.1 10.7 %all-to-all-start.1 = ((f32[8,3,1,1,896]{4,3,2,1,0:T(1,128)}), f32[8,3,1,1,896]{4,3,2,1,0:T(1,128)S(1)}, u32[]{:S(2)}, u32[]{:S(2)}) async-start(f32[8,3,1,1,896]{4,3,2,1,0:T(1,128)} %broadcast_in_dim.117), calls=%async_computation.1 | async-start | bytes 172032 | tf_op jit(solution)/shard_map/all_to_all | solution.py:21
  66.9 8.0 %collective-permute-start.3 = (f32[3,1,8,896]{3,2,0,1:T(8,128)S(1)}, f32[3,1,8,896]{3,2,0,1:T(8,128)S(1)}, u32[]{:S(2)}, u32[]{:S(2)}) collective-permute-start(f32[3,1,8,896]{3,2,0,1:T(8,128)S(1)} %bitcast.551), channel_id=1, source_target_pairs={{8,0},{16,8},{24,16},{32,24},{40,32},{48,40},{56,48},{64,56},{72,6... | collective-permute-start | bytes 258056 | tf_op jit(solution)/shard_map/ppermute | solution.py:36
  70.6 4.3 %collective-permute-start.2 = (f32[3,1,8,896]{3,2,0,1:T(8,128)S(1)}, f32[3,1,8,896]{3,2,0,1:T(8,128)S(1)}, u32[]{:S(2)}, u32[]{:S(2)}) collective-permute-start(f32[3,1,8,896]{3,2,0,1:T(8,128)S(1)} %bitcast.552), channel_id=1, source_target_pairs={{0,8},{8,16},{16,24},{24,32},{32,40},{40,48},{48,56},{56,64},{64,7... | collective-permute-start | bytes 258056 | tf_op jit(solution)/shard_map/ppermute | solution.py:35
  77.3 2.6 %copy-start.5 = (f32[384]{0:T(512)S(1)}, f32[384]{0:T(512)}, u32[]{:S(2)}) copy-start(f32[384]{0:T(512)} %param.34) | copy-start | bytes 4612
  80.8 6.5 %copy-start.3 = (f32[3,512]{1,0:T(4,128)S(1)}, f32[3,512]{1,0:T(4,128)}, u32[]{:S(2)}) copy-start(f32[3,512]{1,0:T(4,128)} %param.31) | copy-start | bytes 18436
  80.8 6.5 %copy-start.6 = (f32[512]{0:T(512)S(1)}, f32[512]{0:T(512)}, u32[]{:S(2)}) copy-start(f32[512]{0:T(512)} %param.32) | copy-start | bytes 6148
  88.7 9.7 %all-to-all-start.5 = ((f32[8,1,7]{2,1,0:T(1,128)}), f32[8,1,7]{2,1,0:T(1,128)S(1)}, u32[]{:S(2)}, u32[]{:S(2)}) async-start(f32[8,1,7]{2,1,0:T(1,128)} %broadcast_in_dim.126), calls=%async_computation.5 | async-start | bytes 8192 | tf_op jit(solution)/shard_map/all_to_all | solution.py:21
  99.1 10.5 %all-to-all-start.4 = ((f32[8,3,1,1,640]{4,3,2,1,0:T(1,128)}), f32[8,3,1,1,640]{4,3,2,1,0:T(1,128)S(1)}, u32[]{:S(2)}, u32[]{:S(2)}) async-start(f32[8,3,1,1,640]{4,3,2,1,0:T(1,128)} %broadcast_in_dim.124), calls=%async_computation.4 | async-start | bytes 122880 | tf_op jit(solution)/shard_map/all_to_all | solution.py:21
  110.2 20.7 %all-to-all-start.6 = ((f32[64,1,7]{2,1,0:T(1,128)}), f32[64,1,7]{2,1,0:T(1,128)S(1)}, u32[]{:S(2)}, u32[]{:S(2)}) async-start(f32[64,1,7]{2,1,0:T(1,128)} %broadcast_in_dim.127), calls=%async_computation.6 | async-start | bytes 65536 | tf_op jit(solution)/shard_map/all_to_all | solution.py:21
  121.6 9.7 %collective-permute-start.5 = (f32[3,1,8,640]{3,2,0,1:T(8,128)S(1)}, f32[3,1,8,640]{3,2,0,1:T(8,128)S(1)}, u32[]{:S(2)}, u32[]{:S(2)}) collective-permute-start(f32[3,1,8,640]{3,2,0,1:T(8,128)S(1)} %bitcast.563), channel_id=1, source_target_pairs={{8,0},{16,8},{24,16},{32,24},{40,32},{48,40},{56,48},{64,56},{72,6... | collective-permute-start | bytes 184328 | tf_op jit(solution)/shard_map/ppermute | solution.py:36
  124.0 7.3 %collective-permute-start.4 = (f32[3,1,8,640]{3,2,0,1:T(8,128)S(1)}, f32[3,1,8,640]{3,2,0,1:T(8,128)S(1)}, u32[]{:S(2)}, u32[]{:S(2)}) collective-permute-start(f32[3,1,8,640]{3,2,0,1:T(8,128)S(1)} %bitcast.564), channel_id=1, source_target_pairs={{0,8},{8,16},{16,24},{24,32},{32,40},{40,48},{48,56},{56,64},{64,7... | collective-permute-start | bytes 184328 | tf_op jit(solution)/shard_map/ppermute | solution.py:35
  144.9 9.7 %all-to-all-start.8 = ((f32[8,1,7]{2,1,0:T(1,128)}), f32[8,1,7]{2,1,0:T(1,128)S(1)}, u32[]{:S(2)}, u32[]{:S(2)}) async-start(f32[8,1,7]{2,1,0:T(1,128)} %broadcast_in_dim.130), calls=%async_computation.8 | async-start | bytes 8192 | tf_op jit(solution)/shard_map/all_to_all | solution.py:21
  155.3 10.6 %all-to-all-start.7 = ((f32[8,3,1,1,640]{4,3,2,1,0:T(1,128)}), f32[8,3,1,1,640]{4,3,2,1,0:T(1,128)S(1)}, u32[]{:S(2)}, u32[]{:S(2)}) async-start(f32[8,3,1,1,640]{4,3,2,1,0:T(1,128)} %broadcast_in_dim.128), calls=%async_computation.7 | async-start | bytes 122880 | tf_op jit(solution)/shard_map/all_to_all | solution.py:21
  166.4 21.1 %all-to-all-start.9 = ((f32[64,1,7]{2,1,0:T(1,128)}), f32[64,1,7]{2,1,0:T(1,128)S(1)}, u32[]{:S(2)}, u32[]{:S(2)}) async-start(f32[64,1,7]{2,1,0:T(1,128)} %broadcast_in_dim.131), calls=%async_computation.9 | async-start | bytes 65536 | tf_op jit(solution)/shard_map/all_to_all | solution.py:21
  178.2 9.7 %collective-permute-start.7 = (f32[3,1,8,640]{3,2,0,1:T(8,128)S(1)}, f32[3,1,8,640]{3,2,0,1:T(8,128)S(1)}, u32[]{:S(2)}, u32[]{:S(2)}) collective-permute-start(f32[3,1,8,640]{3,2,0,1:T(8,128)S(1)} %bitcast.559), channel_id=1, source_target_pairs={{8,0},{16,8},{24,16},{32,24},{40,32},{48,40},{56,48},{64,56},{72,6... | collective-permute-start | bytes 184328 | tf_op jit(solution)/shard_map/ppermute | solution.py:36
  180.6 7.3 %collective-permute-start.6 = (f32[3,1,8,640]{3,2,0,1:T(8,128)S(1)}, f32[3,1,8,640]{3,2,0,1:T(8,128)S(1)}, u32[]{:S(2)}, u32[]{:S(2)}) collective-permute-start(f32[3,1,8,640]{3,2,0,1:T(8,128)S(1)} %bitcast.560), channel_id=1, source_target_pairs={{0,8},{8,16},{16,24},{24,32},{32,40},{40,48},{48,56},{56,64},{64,7... | collective-permute-start | bytes 184328 | tf_op jit(solution)/shard_map/ppermute | solution.py:35
where the time goes:
time: 203 us; the launch traced here: 200 us
  starting transfers between devices  90.3 us (44%)
  waiting for transfers between devices  56 us (28%)
  other arithmetic  30.5 us (15%)
  local copies, waits for them, and re-layouts  20.5 us (10%)
    all_to_all x10, starting transfers between devices, copy_for_each(): return lax.all_to_all(copies, axis, split_axis=0, concat_axis=0, tiled=True)  67.5 us
    all_to_all x10, waiting for transfers between devices, copy_for_each(): return lax.all_to_all(copies, axis, split_axis=0, concat_axis=0, tiled=True)  56 us
    ppermute x4, starting transfers between devices, with_halo(): before = lax.ppermute(last, axis, up)  11.9 us
    ppermute x4, starting transfers between devices, with_halo(): after = lax.ppermute(initial, axis, down)  10.8 us
    reduce_sum x12, other arithmetic, dipole_field(): jnp.sum(radial * delta_x - moments[0][None, :] * direct, axis=1)  10.7 us
    broadcast_in_dim x10, local copies, waits for them, and re-layouts, copy_for_each(): copies = jnp.broadcast_to(x, (lax.axis_size(axis), *x.shape))  6.27 us
    gather x10, local copies, waits for them, and re-layouts, listed_tiles(): taken = jnp.take(tile_set, index_lists, axis=1)  5.42 us
    reduce_sum x9, other arithmetic, dipole_potential(): return jnp.sum(projected * inv_cube, axis=1)  4.73 us
  transfers between devices with their start and end apart: 18, of which 10 were waited for; matrix products, arithmetic and copies ran while one was open for 2% of the time, Pallas kernels for 0%

commit v1 on v0

v1 whole, which is shorter than its diff:
```python
import functools

import jax
import jax.numpy as jnp
from jax import lax
from jax.experimental import pallas as pl
from jax.experimental.pallas import tpu as pltpu
from jax.sharding import PartitionSpec as P

BLOCK = 128
ITERS = 3
CHUNK = 32
SOFT = 0.04
MESH = pl.DeviceIdType.MESH
F32 = jnp.float32


def copy_to(src, dst, send_sem, recv_sem, device):
    pltpu.make_async_remote_copy(
        src_ref=src,
        dst_ref=dst,
        send_sem=send_sem,
        recv_sem=recv_sem,
        device_id=device,
        device_id_type=MESH,
    ).start()


def drain(ref, sem):
    pltpu.make_async_copy(ref, ref, sem).wait()


def powers(dx, dy, dz):
    s = lax.rsqrt(dx * dx + dy * dy + dz * dz + SOFT)
    s2 = s * s
    s3 = s2 * s
    return s3, s3 * s2


def pair_tensor(dx, dy, dz, s3, s5):
    t = 3.0 * s5
    tx, ty, tz = t * dx, t * dy, t * dz
    return (tx * dx - s3, tx * dy, tx * dz, ty * dy - s3, ty * dz, tz * dz - s3)


def kernel(
    ncell, ngrp, lb, lg, nb, nq, nm,
    near_list, grid_list, source_list,
    sites, points, guess, fixed, pol, base, resp,
    out_mu, out_q,
    w0, w1, w2, pos, sa, tb0, tb1, tb2,
    tgt, td, tc, tp, fd, fp, fb, mub, mus, qub, accs, nf, gp,
    send_sem, recv_sem,
):
    windows = (w0, w1, w2)
    tables = (tb0, tb1, tb2)
    cell = lax.axis_index("cell")
    grp = lax.axis_index("grp")
    urows = 3 * lb + lg
    prows = 3 * lb + 3 * lg
    slots = nb + 1
    own = ngrp + grp

    barrier = pltpu.get_barrier_semaphore()

    def greet_far(d, carry):
        pl.semaphore_signal(
            barrier, inc=1, device_id=(lax.rem(cell + d, ncell), grp), device_id_type=MESH
        )
        return carry

    def greet_group(d, carry):
        pl.semaphore_signal(
            barrier, inc=1, device_id=(cell, lax.rem(grp + d, ngrp)), device_id_type=MESH
        )
        return carry

    lax.fori_loop(1, ncell, greet_far, 0)
    lax.fori_loop(1, ngrp, greet_group, 0)

    def lanes(j):
        return pl.ds(j * BLOCK, BLOCK)

    zc = [cell.astype(F32) + 0.5, 0.5, 0.5]
    lane = lax.broadcasted_iota(jnp.int32, (1, BLOCK), 1)

    def put_state(k, mu, q):
        w = windows[k]
        for a in range(3):
            for b in range(lb):
                w[own * urows + a * lb + b] = mu[a][b]
        for g in range(lg):
            w[own * urows + 3 * lb + g] = q[g]
        sums = [functools.reduce(jnp.add, mu[a]) for a in range(3)]
        sums.append(functools.reduce(jnp.add, q))
        for a in range(3):
            moment = functools.reduce(
                jnp.add, [q[g] * (points[a : a + 1, lanes(g)] - zc[a]) for g in range(lg)]
            )
            sums.append(moment + sums[a])
        row = jnp.zeros((1, BLOCK), F32)
        for n, s in enumerate(sums):
            row = jnp.where(lane == n, jnp.sum(s, axis=1, keepdims=True), row)
        sa[k * ngrp + grp] = row

    for a in range(3):
        for b in range(lb):
            pos[own * prows + a * lb + b] = sites[a : a + 1, lanes(b)]
        for g in range(lg):
            pos[own * prows + 3 * lb + a * lg + g] = points[a : a + 1, lanes(g)]
    put_state(
        0,
        [[guess[a : a + 1, lanes(b)] for b in range(lb)] for a in range(3)],
        [base[0:1, lanes(g)] for g in range(lg)],
    )

    def clear(start):
        for w in windows:
            w[pl.ds(start * ngrp * urows, ngrp * urows)] = jnp.zeros(
                (ngrp * urows, 1, BLOCK), F32
            )
        pos[pl.ds(start * ngrp * prows, ngrp * prows)] = jnp.zeros((ngrp * prows, 1, BLOCK), F32)

    @pl.when(cell == 0)
    def _():
        clear(0)

    @pl.when(cell == ncell - 1)
    def _():
        clear(2)

    for a in range(3):
        for b in range(lb):
            tgt[b * 3 + a] = jnp.transpose(
                jnp.broadcast_to(sites[a : a + 1, lanes(b)], (BLOCK, BLOCK))
            )
        for g in range(lg):
            tgt[(lb + g) * 3 + a] = jnp.transpose(
                jnp.broadcast_to(points[a : a + 1, lanes(g)], (BLOCK, BLOCK))
            )

    cells8 = lax.broadcasted_iota(jnp.int32, (8, BLOCK), 0)

    def far_rows(ref, j, c8):
        number = cells8 + c8 * 8
        dx = ref[0:1, lanes(j)] - (number.astype(F32) + 0.5)
        dy = ref[1:2, lanes(j)] - 0.5 + jnp.zeros_like(dx)
        dz = ref[2:3, lanes(j)] - 0.5 + jnp.zeros_like(dx)
        keep = jnp.abs(number - cell) >= 2
        s3, s5 = powers(dx, dy, dz)
        return dx, dy, dz, jnp.where(keep, s3, 0.0), jnp.where(keep, s5, 0.0)

    def far_build(c8, carry):
        row = pl.ds(pl.multiple_of(c8 * 8, 8), 8)
        for b in range(lb):
            dx, dy, dz, s3, s5 = far_rows(sites, b, c8)
            for n, v in enumerate(pair_tensor(dx, dy, dz, s3, s5)):
                fd[b * 9 + n, row] = v
            for n, v in enumerate((dx, dy, dz)):
                fd[b * 9 + 6 + n, row] = v * s3
        for g in range(lg):
            dx, dy, dz, s3, s5 = far_rows(points, g, c8)
            for n, v in enumerate((dx, dy, dz)):
                fp[g * 3 + n, row] = v * s3
        return carry

    lax.fori_loop(0, ncell // 8, far_build, 0)

    pl.semaphore_wait(barrier, ncell + ngrp - 2)

    S_SA, S_W, S_FL, S_FR, S_TB = 0, 3, 6, 9, 12
    S_POS, S_PL, S_PR = 15, 16, 17

    def share_group(ref, start, count, sem):
        def step(d, carry):
            part = ref.at[pl.ds(start, count)]
            copy_to(
                part, part, send_sem.at[sem], recv_sem.at[sem], (cell, lax.rem(grp + d, ngrp))
            )
            return carry

        lax.fori_loop(1, ngrp, step, 0)

    def share_sums(k):
        share_group(sa, k * ngrp + grp, 1, S_SA + k)

    def share_state(k):
        share_group(windows[k], own * urows, urows, S_W + k)

    def share_cell(k):
        drain(sa.at[pl.ds(0, ngrp - 1)], recv_sem.at[S_SA + k])
        total = functools.reduce(jnp.add, [sa[k * ngrp + j] for j in range(ngrp)])
        table = tables[k]
        table[cell] = total

        def step(d, carry):
            part = table.at[pl.ds(cell, 1)]
            copy_to(
                part,
                part,
                send_sem.at[S_TB + k],
                recv_sem.at[S_TB + k],
                (lax.rem(cell + d, ncell), grp),
            )
            return carry

        lax.fori_loop(1, ncell, step, 0)

    def forward(ref, rows, sem_group, sem_left, sem_right):
        drain(ref.at[pl.ds(0, (ngrp - 1) * rows)], recv_sem.at[sem_group])
        size = ngrp * rows
        mine = ref.at[pl.ds(size, size)]

        @pl.when(cell < ncell - 1)
        def _():
            copy_to(
                mine, ref.at[pl.ds(0, size)],
                send_sem.at[sem_right], recv_sem.at[sem_right], (cell + 1, grp),
            )

        @pl.when(cell > 0)
        def _():
            copy_to(
                mine, ref.at[pl.ds(2 * size, size)],
                send_sem.at[sem_left], recv_sem.at[sem_left], (cell - 1, grp),
            )

    def arrived(ref, rows, sem_left, sem_right):
        size = ngrp * rows

        @pl.when(cell > 0)
        def _():
            drain(ref.at[pl.ds(0, size)], recv_sem.at[sem_right])

        @pl.when(cell < ncell - 1)
        def _():
            drain(ref.at[pl.ds(2 * size, size)], recv_sem.at[sem_left])

    def block_row(w, rows, offset):
        return (w // lb) * rows + lax.rem(w, lb) + offset

    def point_row(w, rows, offset):
        return (w // lg) * rows + lax.rem(w, lg) + offset

    def source_slot(b, s):
        return (ngrp + grp) * lb + b if s == 0 else near_list[b, s - 1]

    def build():
        diagonal = (
            lax.broadcasted_iota(jnp.int32, (CHUNK, BLOCK), 1)
            - lax.broadcasted_iota(jnp.int32, (CHUNK, BLOCK), 0)
        )

        def deltas(t, j, rows):
            row = pl.ds(pl.multiple_of(t * CHUNK, CHUNK), CHUNK)
            return row, [tgt[j * 3 + a, row] - rows[a] for a in range(3)]

        def atoms(b, carry):
            for s in range(slots):
                r = block_row(source_slot(b, s), prows, 0)
                rows = [pos[r + a * lb] for a in range(3)]

                def step(t, c, s=s, rows=rows):
                    row, (dx, dy, dz) = deltas(t, b, rows)
                    s3, s5 = powers(dx, dy, dz)
                    if s == 0:
                        s3 = jnp.where(diagonal == t * CHUNK, 0.0, s3)
                    for n, v in enumerate(pair_tensor(dx, dy, dz, s3, s5)):
                        td[(b * slots + s) * 6 + n, row] = v
                    return c

                lax.fori_loop(0, BLOCK // CHUNK, step, 0)
            for s in range(nq):
                r = point_row(grid_list[b, s], prows, 3 * lb)
                rows = [pos[r + a * lg] for a in range(3)]

                def step(t, c, s=s, rows=rows):
                    row, (dx, dy, dz) = deltas(t, b, rows)
                    s3, s5 = powers(dx, dy, dz)
                    for n, v in enumerate((dx, dy, dz)):
                        tc[(b * nq + s) * 3 + n, row] = v * s3
                    return c

                lax.fori_loop(0, BLOCK // CHUNK, step, 0)
            return carry

        lax.fori_loop(0, lb, atoms, 0)

        def grids(g, carry):
            for s in range(nm):
                r = block_row(source_list[g, s], prows, 0)
                rows = [pos[r + a * lb] for a in range(3)]

                def step(t, c, s=s, rows=rows):
                    row, (dx, dy, dz) = deltas(t, lb + g, rows)
                    s3, s5 = powers(dx, dy, dz)
                    for n, v in enumerate((dx, dy, dz)):
                        tp[(g * nm + s) * 3 + n, row] = v * s3
                    return c

                lax.fori_loop(0, BLOCK // CHUNK, step, 0)
            return carry

        lax.fori_loop(0, lg, grids, 0)

    def apply_near(w):
        def wide(row):
            return jnp.broadcast_to(row, (8, BLOCK))

        def pick_atoms(b, carry):
            for s in range(slots):
                r = block_row(source_slot(b, s), urows, 0)
                for a in range(3):
                    mub[(b * slots + s) * 3 + a] = wide(w[r + a * lb])
            for s in range(nq):
                qub[b * nq + s] = wide(w[point_row(grid_list[b, s], urows, 3 * lb)])
            return carry

        lax.fori_loop(0, lb, pick_atoms, 0)

        def pick_grids(g, carry):
            for s in range(nm):
                r = block_row(source_list[g, s], urows, 0)
                for a in range(3):
                    mus[(g * nm + s) * 3 + a] = wide(w[r + a * lb])
            return carry

        lax.fori_loop(0, lg, pick_grids, 0)

        parts = CHUNK // 8

        def atoms(j, carry):
            b = j // (BLOCK // CHUNK)
            start = lax.rem(j, BLOCK // CHUNK) * CHUNK
            rows = [pl.ds(pl.multiple_of(start + 8 * i, 8), 8) for i in range(parts)]
            acc = [[jnp.zeros((8, BLOCK), F32) for _ in range(parts)] for _ in range(3)]
            for s in range(slots):
                mx, my, mz = [mub[(b * slots + s) * 3 + a] for a in range(3)]
                at = (b * slots + s) * 6
                for i in range(parts):
                    xx, xy, xz, yy, yz, zz = [td[at + n, rows[i]] for n in range(6)]
                    acc[0][i] = acc[0][i] + (xx * mx + xy * my + xz * mz)
                    acc[1][i] = acc[1][i] + (xy * mx + yy * my + yz * mz)
                    acc[2][i] = acc[2][i] + (xz * mx + yz * my + zz * mz)
            for s in range(nq):
                q = qub[b * nq + s]
                for i in range(parts):
                    for a in range(3):
                        acc[a][i] = acc[a][i] + tc[(b * nq + s) * 3 + a, rows[i]] * q
            for a in range(3):
                for i in range(parts):
                    accs[b * 3 + a, rows[i]] = acc[a][i]
            return carry

        lax.fori_loop(0, lb * (BLOCK // CHUNK), atoms, 0)

        def grids(j, carry):
            g = j // (BLOCK // CHUNK)
            start = lax.rem(j, BLOCK // CHUNK) * CHUNK
            rows = [pl.ds(pl.multiple_of(start + 8 * i, 8), 8) for i in range(parts)]
            acc = [jnp.zeros((8, BLOCK), F32) for _ in range(parts)]
            for s in range(nm):
                m = [mus[(g * nm + s) * 3 + a] for a in range(3)]
                at = (g * nm + s) * 3
                for i in range(parts):
                    acc[i] = acc[i] + (
                        tp[at, rows[i]] * m[0] + tp[at + 1, rows[i]] * m[1]
                        + tp[at + 2, rows[i]] * m[2]
                    )
            for i in range(parts):
                accs[3 * lb + g, rows[i]] = acc[i]
            return carry

        lax.fori_loop(0, lg * (BLOCK // CHUNK), grids, 0)

        for j in range(3 * lb + lg):
            nf[j] = jnp.sum(jnp.transpose(accs[j]), axis=0, keepdims=True)

    def apply_far(k):
        table = tables[k]
        drain(table.at[pl.ds(0, ncell - 1)], recv_sem.at[S_TB + k])
        for c8 in range(ncell // 8):
            rows = table[pl.ds(c8 * 8, 8)].reshape(8, BLOCK)
            for n in range(7):
                fb[n, pl.ds(c8 * 8, 8)] = jnp.broadcast_to(rows[:, n : n + 1], (8, BLOCK))
        field = [[None] * lb for _ in range(3)]
        for b in range(lb):
            acc = [jnp.zeros((8, BLOCK), F32) for _ in range(3)]
            for c8 in range(ncell // 8):
                row = pl.ds(c8 * 8, 8)
                xx, xy, xz, yy, yz, zz, cx, cy, cz = [fd[b * 9 + n, row] for n in range(9)]
                q, mx, my, mz = [fb[n, row] for n in range(3, 7)]
                acc[0] = acc[0] + ((xx * mx + xy * my) + (xz * mz + cx * q))
                acc[1] = acc[1] + ((xy * mx + yy * my) + (yz * mz + cy * q))
                acc[2] = acc[2] + ((xz * mx + yz * my) + (zz * mz + cz * q))
            for a in range(3):
                field[a][b] = jnp.sum(acc[a], axis=0, keepdims=True) + nf[b * 3 + a]
        potential = []
        for g in range(lg):
            acc = jnp.zeros((8, BLOCK), F32)
            for c8 in range(ncell // 8):
                row = pl.ds(c8 * 8, 8)
                acc = acc + (
                    fp[g * 3, row] * fb[0, row] + fp[g * 3 + 1, row] * fb[1, row]
                    + fp[g * 3 + 2, row] * fb[2, row]
                )
            potential.append(jnp.sum(acc, axis=0, keepdims=True) + nf[3 * lb + g])
        mu = [
            [pol[0:1, lanes(b)] * (fixed[a : a + 1, lanes(b)] + field[a][b]) for b in range(lb)]
            for a in range(3)
        ]
        q = [base[0:1, lanes(g)] - resp[0:1, lanes(g)] * potential[g] for g in range(lg)]
        return mu, q

    share_sums(0)
    share_group(pos, own * prows, prows, S_POS)
    share_state(0)
    for k in range(ITERS):
        share_cell(k)
        if k == 0:
            forward(pos, prows, S_POS, S_PL, S_PR)
        forward(windows[k], urows, S_W + k, S_FL + k, S_FR + k)
        if k == 0:
            arrived(pos, prows, S_PL, S_PR)
            build()
        arrived(windows[k], urows, S_FL + k, S_FR + k)
        apply_near(windows[k])
        mu, q = apply_far(k)
        if k < ITERS - 1:
            put_state(k + 1, mu, q)
            share_sums(k + 1)
            share_state(k + 1)
        else:
            for a in range(3):
                for b in range(lb):
                    out_mu[a : a + 1, lanes(b)] = mu[a][b]
            for g in range(lg):
                out_q[0:1, lanes(g)] = q[g]

    def sent(ref, rows, sem_group, sem_left, sem_right):
        size = ngrp * rows
        drain(ref.at[pl.ds(0, (ngrp - 1) * rows)], send_sem.at[sem_group])

        @pl.when(cell < ncell - 1)
        def _():
            drain(ref.at[pl.ds(0, size)], send_sem.at[sem_right])

        @pl.when(cell > 0)
        def _():
            drain(ref.at[pl.ds(0, size)], send_sem.at[sem_left])

    sent(pos, prows, S_POS, S_PL, S_PR)
    for k in range(ITERS):
        drain(sa.at[pl.ds(0, ngrp - 1)], send_sem.at[S_SA + k])
        drain(tables[k].at[pl.ds(0, ncell - 1)], send_sem.at[S_TB + k])
        sent(windows[k], urows, S_W + k, S_FL + k, S_FR + k)


def body(
    ncell, ngrp,
    atom_sites, grid_points, dipole_guess, fixed_field, polarisability, base_charge, response,
    near_blocks, grid_blocks, source_blocks,
):
    lb, nb = near_blocks.shape
    nq = grid_blocks.shape[1]
    lg, nm = source_blocks.shape
    urows = 3 * lb + lg
    prows = 3 * lb + 3 * lg
    vmem = pl.BlockSpec(memory_space=pltpu.VMEM)
    smem = pl.BlockSpec(memory_space=pltpu.SMEM)
    tile = (BLOCK, BLOCK)
    window = pltpu.VMEM((3 * ngrp * urows, 1, BLOCK), F32)
    table = pltpu.VMEM((ncell, 1, BLOCK), F32)
    mu, q = pl.pallas_call(
        functools.partial(kernel, ncell, ngrp, lb, lg, nb, nq, nm),
        out_shape=(
            jax.ShapeDtypeStruct((3, lb * BLOCK), F32),
            jax.ShapeDtypeStruct((1, lg * BLOCK), F32),
        ),
        in_specs=[smem] * 3 + [vmem] * 7,
        out_specs=(vmem, vmem),
        scratch_shapes=[
            window, window, window,
            pltpu.VMEM((3 * ngrp * prows, 1, BLOCK), F32),
            pltpu.VMEM((ITERS * ngrp, 1, BLOCK), F32),
            table, table, table,
            pltpu.VMEM(((lb + lg) * 3, *tile), F32),
            pltpu.VMEM((lb * (nb + 1) * 6, *tile), F32),
            pltpu.VMEM((lb * nq * 3, *tile), F32),
            pltpu.VMEM((lg * nm * 3, *tile), F32),
            pltpu.VMEM((lb * 9, ncell, BLOCK), F32),
            pltpu.VMEM((lg * 3, ncell, BLOCK), F32),
            pltpu.VMEM((7, ncell, BLOCK), F32),
            pltpu.VMEM((lb * (nb + 1) * 3, 8, BLOCK), F32),
            pltpu.VMEM((lg * nm * 3, 8, BLOCK), F32),
            pltpu.VMEM((lb * nq, 8, BLOCK), F32),
            pltpu.VMEM((3 * lb + lg, *tile), F32),
            pltpu.VMEM((3 * lb + lg, 1, BLOCK), F32),
            pltpu.VMEM((8, BLOCK), F32),
            pltpu.SemaphoreType.DMA((18,)),
            pltpu.SemaphoreType.DMA((18,)),
        ],
        compiler_params=pltpu.CompilerParams(
            collective_id=0, has_side_effects=True, vmem_limit_bytes=60 * 1024 * 1024
        ),
    )(
        near_blocks, grid_blocks, source_blocks,
        atom_sites, grid_points, dipole_guess, fixed_field,
        polarisability.reshape(1, -1), base_charge.reshape(1, -1), response.reshape(1, -1),
    )
    return mu, q.reshape(-1)


def solution(mesh):
    shared = P(None, ("cell", "grp"))
    flat = P(("cell", "grp"))
    rows = P(("cell", "grp"), None)
    return jax.shard_map(
        functools.partial(body, mesh.shape["cell"], mesh.shape["grp"]),
        mesh=mesh,
        in_specs=(shared, shared, shared, shared, flat, flat, flat, rows, rows, rows),
        out_specs=(shared, flat),
        check_vma=False,
    )
```

time: 203 us -> 70.8 us (0.35); the launches traced: 200 us -> 70.5 us
  starting transfers between devices: 90.3 us -> 0 us
  Pallas kernels: 0 us -> 65.5 us
  waiting for transfers between devices: 56 us -> 0 us
  other arithmetic: 30.5 us -> 0.6 us
  local copies, waits for them, and re-layouts: 20.5 us -> 3.76 us
    all_to_all x10 -> x0, starting transfers between devices: 67.5 us -> none  [copy_for_each(): return lax.all_to_all(copies, axis, split_axis=0, concat_axis=0, tiled=True)]
    pallas_call x0 -> x1, Pallas kernels: none -> 65.5 us  [body(): pl.pallas_call(functools.partial(kernel, ncell, ngrp, lb, lg, nb, nq, nm)...]
    all_to_all x10 -> x0, waiting for transfers between devices: 56 us -> none  [copy_for_each(): return lax.all_to_all(copies, axis, split_axis=0, concat_axis=0, tiled=True)]
    reduce_sum x66 -> x0, other arithmetic: 25.1 us -> none  [the longest x12 10.7 us: dipole_field(): jnp.sum(radial * delta_x - moments[0][None, :] * direct, axis=1)]
    ppermute x8 -> x0, starting transfers between devices: 22.7 us -> none  [the longest x4 11.9 us: with_halo(): before = lax.ppermute(last, axis, up)]
    gather x13 -> x0, local copies, waits for them, and re-layouts: 7.11 us -> none  [the longest x10 5.42 us: listed_tiles(): taken = jnp.take(tile_set, index_lists, axis=1)]
    broadcast_in_dim x13 -> x0, local copies, waits for them, and re-layouts: 6.52 us -> none  [the longest x10 6.27 us: copy_for_each(): copies = jnp.broadcast_to(x, (lax.axis_size(axis), *x.shape))]
    concatenate x11 -> x0, other arithmetic: 2.29 us -> none  [the longest x3 2.16 us: body(): jnp.concatenate([jnp.sum(dipoles, axis=1), jnp.sum(charges)[None], jnp.su...]
  transfers between devices with their start and end apart: 18 -> 0, of which waited for: 10 -> 0; matrix products, arithmetic and copies ran while one was open for 2% -> 0% of each run, Pallas kernels for 0% -> 0%
where the time goes in v1:
time: 70.8 us; the launch traced here: 70.5 us
  Pallas kernels  65.5 us (93%)
  local copies, waits for them, and re-layouts  3.76 us (5%)
    pallas_call x1, Pallas kernels, body(): pl.pallas_call(functools.partial(kernel, ncell, ngrp, lb, lg, nb, nq, nm)...  65.5 us
    unnamed x5, local copies, waits for them, and re-layouts  1.95 us

profile of v1, /device:TPU:1, one launch (start us, length us, event | category | flops | bytes accessed | tf_op | source)
XLA Modules:
  0.0 70.5 jit_solution(1832726770178511641)
XLA Ops:
  0.6 0.0 copy-start
  0.6 1.3 %reshape.17.base = f32[1,384]{1,0:T(1,128)} reshape(f32[384]{0:T(512)} %param.15) | data formatting | bytes 3072 | tf_op jit(solution)/shard_map/reshape | solution.py:509
  1.9 0.0 copy-done
  1.9 0.6 reshape.18.resp
  2.5 65.5 %shard_map.113 = (f32[3,512]{1,0:T(4,128)}, f32[1,384]{1,0:T(1,128)}) custom-call(s32[4,8]{1,0:T(4,128)} %near_list.1, s32[4,4]{1,0:T(4,128)} %grid_list.1, s32[3,8]{1,0:T(4,128)} %source_list.1, f32[3,512]{1,0:T(4,128)} %sites.1, f32[3,384]{1,0:T(4,128)} %points.1, f32[3,512]{1,0:T(4,128)} %guess.1, f32[3,512]{1,0:T(4,128)} %fixed.1, f32[1,512]{1,0:T(1,128)} %bitcast.1, ...), custom_call_target="tpu_custom_call" | custom-call | tf_op jit(solution)/shard_map/pallas_call | solution.py:474
  68.0 0.0 copy-start.1
  68.0 0.6 copy-done.1
  68.7 0.6 reduce
  69.2 1.3 %copy.13 = f32[3,512]{1,0:T(4,128)} copy(f32[3,512]{1,0:T(4,128)} %get-tuple-element.8) | data formatting | bytes 12288
Async XLA Ops:
  0.6 1.3 %copy-start = (f32[384]{0:T(512)S(1)}, f32[384]{0:T(512)}, u32[]{:S(2)}) copy-start(f32[384]{0:T(512)} %param.16) | copy-start | bytes 4612
  68.0 0.7 copy-start.1

commit v2 on v1

v2 whole, which is shorter than its diff:
```python
import functools

import jax
import jax.numpy as jnp
from jax import lax
from jax.experimental import pallas as pl
from jax.experimental.pallas import tpu as pltpu
from jax.sharding import PartitionSpec as P

BLOCK = 128
ITERS = 3
CHUNK = 32
SOFT = 0.04
ROOT3 = 3.0**0.5
MESH = pl.DeviceIdType.MESH
F32 = jnp.float32


def copy_to(src, dst, send_sem, recv_sem, device):
    pltpu.make_async_remote_copy(
        src_ref=src,
        dst_ref=dst,
        send_sem=send_sem,
        recv_sem=recv_sem,
        device_id=device,
        device_id_type=MESH,
    ).start()


def drain(ref, sem):
    pltpu.make_async_copy(ref, ref, sem).wait()


def ring_order(size):
    return sorted(range(1, size), key=lambda d: -min(d, size - d))


def far_order(ncell):
    def hops(d):
        total = 0
        for c in range(ncell):
            a, b = c // 2, (c + d) % ncell // 2
            dz, dx = abs(a % 8 - b % 8), abs(a // 8 - b // 8)
            total += min(dz, 8 - dz) + min(dx, ncell // 16 - dx)
        return total

    return sorted(range(1, ncell), key=lambda d: (-hops(d), d))


def powers(dx, dy, dz):
    s = lax.rsqrt(dx * dx + dy * dy + dz * dz + SOFT)
    return s, s * s * s


def pair_tensor(dx, dy, dz, s3, s5):
    t = 3.0 * s5
    tx, ty, tz = t * dx, t * dy, t * dz
    return (tx * dx - s3, tx * dy, tx * dz, ty * dy - s3, ty * dz, tz * dz - s3)


def kernel(
    ncell, ngrp, lb, lg, nb, nq, nm,
    near_in, grid_in, source_in,
    sites_in, points_in, guess_in, fixed_in, pol_in, base_in, resp_in,
    out_mu, out_q,
    near_list, grid_list, source_list,
    sites, points, guess, fixed, pol, base, resp,
    urow, prow,
    w0, w1, w2, pos, sa, tb0, tb1, tb2,
    tgt, td, tc, tp, fd, fp, fb, mub, accs, nf,
    local_sem, send_sem, recv_sem,
):
    windows = (w0, w1, w2)
    tables = (tb0, tb1, tb2)
    cell = lax.axis_index("cell")
    grp = lax.axis_index("grp")
    urows = 3 * lb + lg
    prows = 3 * lb + 3 * lg
    slots = nb + 1
    own = ngrp + grp

    loads = [
        pltpu.make_async_copy(src, dst, local_sem.at[n])
        for n, (src, dst) in enumerate(
            (
                (sites_in, sites), (points_in, points), (guess_in, guess), (base_in, base),
                (near_in, near_list), (grid_in, grid_list), (source_in, source_list),
                (fixed_in, fixed), (pol_in, pol), (resp_in, resp),
            )
        )
    ]
    for load in loads:
        load.start()
    others = far_order(ncell)

    def cell_at(d):
        return (cell + d) & (ncell - 1)

    def group_at(d):
        return (grp + d) & (ngrp - 1)

    barrier = pltpu.get_barrier_semaphore()
    with jax.named_scope("greet"):
        for d in others:
            pl.semaphore_signal(
                barrier, inc=1, device_id=(cell_at(d), grp), device_id_type=MESH
            )
        for d in ring_order(ngrp):
            pl.semaphore_signal(
                barrier, inc=1, device_id=(cell, group_at(d)), device_id_type=MESH
            )
    for load in loads:
        load.wait()

    def lanes(j):
        return pl.ds(j * BLOCK, BLOCK)

    zc = [cell.astype(F32) + 0.5, 0.5, 0.5]
    lane = lax.broadcasted_iota(jnp.int32, (1, BLOCK), 1)

    def put_state(k, mu, q):
        w = windows[k]
        for a in range(3):
            for b in range(lb):
                w[own * urows + a * lb + b] = mu[a][b]
        for g in range(lg):
            w[own * urows + 3 * lb + g] = q[g]
        sums = [functools.reduce(jnp.add, mu[a]) for a in range(3)]
        sums.append(functools.reduce(jnp.add, q))
        for a in range(3):
            moment = functools.reduce(
                jnp.add, [q[g] * (points[a : a + 1, lanes(g)] - zc[a]) for g in range(lg)]
            )
            sums.append(moment + sums[a])
        row = jnp.zeros((1, BLOCK), F32)
        for n, s in enumerate(sums):
            row = jnp.where(lane == n, jnp.sum(s, axis=1, keepdims=True), row)
        sa[k * ngrp + grp] = row

    for a in range(3):
        for b in range(lb):
            pos[own * prows + a * lb + b] = sites[a : a + 1, lanes(b)]
        for g in range(lg):
            pos[own * prows + 3 * lb + a * lg + g] = points[a : a + 1, lanes(g)]
    put_state(
        0,
        [[guess[a : a + 1, lanes(b)] for b in range(lb)] for a in range(3)],
        [base[g : g + 1] for g in range(lg)],
    )

    def atom_rows(n, w):
        at, b = lax.shift_right_logical(w, lb.bit_length() - 1), w & (lb - 1)
        urow[n] = at * urows + b
        prow[n] = at * prows + b

    def grid_rows(n, w):
        at = w // lg
        b = w - at * lg
        urow[n] = at * urows + 3 * lb + b
        prow[n] = at * prows + 3 * lb + b

    A_GRID = lb * slots
    A_SRC = A_GRID + lb * nq
    for b in range(lb):
        atom_rows(b * slots, own * lb + b)
        for s in range(nb):
            atom_rows(b * slots + 1 + s, near_list[b, s])
        for s in range(nq):
            grid_rows(A_GRID + b * nq + s, grid_list[b, s])
    for g in range(lg):
        for s in range(nm):
            atom_rows(A_SRC + g * nm + s, source_list[g, s])

    def clear(start):
        for w in windows:
            w[pl.ds(start * ngrp * urows, ngrp * urows)] = jnp.zeros(
                (ngrp * urows, 1, BLOCK), F32
            )
        pos[pl.ds(start * ngrp * prows, ngrp * prows)] = jnp.zeros((ngrp * prows, 1, BLOCK), F32)

    @pl.when(cell == 0)
    def _():
        clear(0)

    @pl.when(cell == ncell - 1)
    def _():
        clear(2)

    for a in range(3):
        for b in range(lb):
            tgt[b * 3 + a] = jnp.transpose(
                jnp.broadcast_to(sites[a : a + 1, lanes(b)], (BLOCK, BLOCK))
            )
        for g in range(lg):
            tgt[(lb + g) * 3 + a] = jnp.transpose(
                jnp.broadcast_to(points[a : a + 1, lanes(g)], (BLOCK, BLOCK))
            )

    cells8 = lax.broadcasted_iota(jnp.int32, (8, BLOCK), 0)

    def far_rows(ref, j, c8):
        number = cells8 + c8 * 8
        dx = ref[0:1, lanes(j)] - (number.astype(F32) + 0.5)
        dy = ref[1:2, lanes(j)] - 0.5 + jnp.zeros_like(dx)
        dz = ref[2:3, lanes(j)] - 0.5 + jnp.zeros_like(dx)
        keep = jnp.abs(number - cell) >= 2
        s1, s3 = powers(dx, dy, dz)
        s3 = jnp.where(keep, s3, 0.0)
        return dx, dy, dz, s3, s3 * s1 * s1

    def far_build(c8, carry):
        row = pl.ds(pl.multiple_of(c8 * 8, 8), 8)
        for b in range(lb):
            dx, dy, dz, s3, s5 = far_rows(sites, b, c8)
            for n, v in enumerate(pair_tensor(dx, dy, dz, s3, s5)):
                fd[b * 9 + n, row] = v
            for n, v in enumerate((dx, dy, dz)):
                fd[b * 9 + 6 + n, row] = v * s3
        for g in range(lg):
            dx, dy, dz, s3, s5 = far_rows(points, g, c8)
            for n, v in enumerate((dx, dy, dz)):
                fp[g * 3 + n, row] = v * s3
        return carry

    with jax.named_scope("far_build"):
        lax.fori_loop(0, ncell // 8, far_build, 0)

    with jax.named_scope("barrier"):
        pl.semaphore_wait(barrier, ncell + ngrp - 2)

    S_SA, S_W, S_FL, S_FR, S_TB = 0, 3, 6, 9, 12
    S_POS, S_PL, S_PR = 15, 16, 17

    def share_group(ref, start, count, sem):
        part = ref.at[pl.ds(start, count)]
        for d in ring_order(ngrp):
            copy_to(part, part, send_sem.at[sem], recv_sem.at[sem], (cell, group_at(d)))

    def share_sums(k):
        share_group(sa, k * ngrp + grp, 1, S_SA + k)

    def share_state(k):
        share_group(windows[k], own * urows, urows, S_W + k)

    def share_cell(k):
        drain(sa.at[pl.ds(0, ngrp - 1)], recv_sem.at[S_SA + k])
        total = functools.reduce(jnp.add, [sa[k * ngrp + j] for j in range(ngrp)])
        table = tables[k]
        table[cell] = total

        part = table.at[pl.ds(cell, 1)]
        for d in others:
            copy_to(
                part, part, send_sem.at[S_TB + k], recv_sem.at[S_TB + k], (cell_at(d), grp)
            )

    def forward(ref, rows, sem_group, sem_left, sem_right):
        drain(ref.at[pl.ds(0, (ngrp - 1) * rows)], recv_sem.at[sem_group])
        size = ngrp * rows
        mine = ref.at[pl.ds(size, size)]

        @pl.when(cell < ncell - 1)
        def _():
            copy_to(
                mine, ref.at[pl.ds(0, size)],
                send_sem.at[sem_right], recv_sem.at[sem_right], (cell + 1, grp),
            )

        @pl.when(cell > 0)
        def _():
            copy_to(
                mine, ref.at[pl.ds(2 * size, size)],
                send_sem.at[sem_left], recv_sem.at[sem_left], (cell - 1, grp),
            )

    def arrived(ref, rows, sem_left, sem_right):
        size = ngrp * rows

        @pl.when(cell > 0)
        def _():
            drain(ref.at[pl.ds(0, size)], recv_sem.at[sem_right])

        @pl.when(cell < ncell - 1)
        def _():
            drain(ref.at[pl.ds(2 * size, size)], recv_sem.at[sem_left])

    tiles = BLOCK // 8

    def tile(t):
        return pl.ds(8 * t, 8)

    def wide(row):
        return jnp.broadcast_to(row, (8, BLOCK))

    def build():
        diagonal = lax.broadcasted_iota(jnp.int32, (8, BLOCK), 1) - lax.broadcasted_iota(
            jnp.int32, (8, BLOCK), 0
        )

        def deltas(j, t, rows):
            return [tgt[j * 3 + a, tile(t)] - rows[a] for a in range(3)]

        def dipole_slot(b, n, own_block):
            r = prow[n]
            rows = [wide(pos[r + a * lb]) for a in range(3)]
            for t in range(tiles):
                dx, dy, dz = deltas(b, t, rows)
                s1, s3 = powers(dx, dy, dz)
                w = ROOT3 * (s3 * lax.rsqrt(s1))
                if own_block:
                    s3 = jnp.where(diagonal == 8 * t, 0.0, s3)
                for i, v in enumerate((w * dx, w * dy, w * dz, s3)):
                    td[n * 4 + i, tile(t)] = v

        def charge_slot(ref, j, n, at, step):
            r = prow[n]
            rows = [wide(pos[r + a * step]) for a in range(3)]
            for t in range(tiles):
                dx, dy, dz = deltas(j, t, rows)
                _, s3 = powers(dx, dy, dz)
                for i, v in enumerate((dx, dy, dz)):
                    ref[at * 3 + i, tile(t)] = v * s3

        def atoms(b, carry):
            dipole_slot(b, b * slots, True)

            def pair(i, c):
                dipole_slot(b, b * slots + 1 + 2 * i, False)
                dipole_slot(b, b * slots + 2 + 2 * i, False)
                return c

            lax.fori_loop(0, nb // 2, pair, 0)

            def charge(i, c):
                for e in range(2):
                    at = b * nq + 2 * i + e
                    charge_slot(tc, b, A_GRID + at, at, lg)
                return c

            lax.fori_loop(0, nq // 2, charge, 0)
            return carry

        lax.fori_loop(0, lb, atoms, 0)

        def grids(i, carry):
            g = i // (nm // 2)
            for e in range(2):
                at = 2 * i + e
                charge_slot(tp, lb + g, A_SRC + at, at, lb)
            return carry

        lax.fori_loop(0, lg * nm // 2, grids, 0)

    def reduce_rows(j):
        nf[j] = jnp.sum(jnp.transpose(accs[j]), axis=0, keepdims=True)

    def apply_near(w):
        parts = CHUNK // 8

        def atoms(b, carry):
            for s in range(slots):
                r = urow[b * slots + s]
                for a in range(3):
                    mub[s * 3 + a] = wide(w[r + a * lb])
            for s in range(nq):
                mub[slots * 3 + s] = wide(w[urow[A_GRID + b * nq + s]])
            before = jnp.maximum(b - 1, 0)
            for c in range(BLOCK // CHUNK):
                rows = [tile(c * parts + i) for i in range(parts)]
                acc = [[jnp.zeros((8, BLOCK), F32) for _ in range(parts)] for _ in range(3)]
                for s in range(slots):
                    m = [mub[s * 3 + a] for a in range(3)]
                    at = (b * slots + s) * 4
                    for i in range(parts):
                        vx, vy, vz, s3 = [td[at + n, rows[i]] for n in range(4)]
                        p = vx * m[0] + vy * m[1] + vz * m[2]
                        for a, v in enumerate((vx, vy, vz)):
                            acc[a][i] = acc[a][i] + (v * p - s3 * m[a])
                for s in range(nq):
                    q = mub[slots * 3 + s]
                    for i in range(parts):
                        for a in range(3):
                            acc[a][i] = acc[a][i] + tc[(b * nq + s) * 3 + a, rows[i]] * q
                for a in range(3):
                    for i in range(parts):
                        accs[b * 3 + a, rows[i]] = acc[a][i]
                if c < 3:
                    reduce_rows(before * 3 + c)
            return carry

        lax.fori_loop(0, lb, atoms, 0)

        def grids(g, carry):
            for s in range(nm):
                r = urow[A_SRC + g * nm + s]
                for a in range(3):
                    mub[s * 3 + a] = wide(w[r + a * lb])
            for c in range(BLOCK // CHUNK):
                rows = [tile(c * parts + i) for i in range(parts)]
                acc = [jnp.zeros((8, BLOCK), F32) for _ in range(parts)]
                for s in range(nm):
                    m = [mub[s * 3 + a] for a in range(3)]
                    at = (g * nm + s) * 3
                    for i in range(parts):
                        acc[i] = acc[i] + (
                            tp[at, rows[i]] * m[0] + tp[at + 1, rows[i]] * m[1]
                            + tp[at + 2, rows[i]] * m[2]
                        )
                for i in range(parts):
                    accs[3 * lb + g, rows[i]] = acc[i]
            reduce_rows(3 * lb - 3 + g)
            return carry

        lax.fori_loop(0, lg, grids, 0)
        for g in range(lg):
            reduce_rows(3 * lb + g)

    def apply_far(k):
        table = tables[k]
        for c8 in range(ncell // 8):
            rows = table[pl.ds(c8 * 8, 8)].reshape(8, BLOCK)
            for n in range(7):
                fb[n, pl.ds(c8 * 8, 8)] = jnp.broadcast_to(rows[:, n : n + 1], (8, BLOCK))
        field = [[None] * lb for _ in range(3)]
        for b in range(lb):
            acc = [jnp.zeros((8, BLOCK), F32) for _ in range(3)]
            for c8 in range(ncell // 8):
                row = pl.ds(c8 * 8, 8)
                xx, xy, xz, yy, yz, zz, cx, cy, cz = [fd[b * 9 + n, row] for n in range(9)]
                q, mx, my, mz = [fb[n, row] for n in range(3, 7)]
                acc[0] = acc[0] + ((xx * mx + xy * my) + (xz * mz + cx * q))
                acc[1] = acc[1] + ((xy * mx + yy * my) + (yz * mz + cy * q))
                acc[2] = acc[2] + ((xz * mx + yz * my) + (zz * mz + cz * q))
            for a in range(3):
                field[a][b] = jnp.sum(acc[a], axis=0, keepdims=True) + nf[b * 3 + a]
        potential = []
        for g in range(lg):
            acc = jnp.zeros((8, BLOCK), F32)
            for c8 in range(ncell // 8):
                row = pl.ds(c8 * 8, 8)
                acc = acc + (
                    fp[g * 3, row] * fb[0, row] + fp[g * 3 + 1, row] * fb[1, row]
                    + fp[g * 3 + 2, row] * fb[2, row]
                )
            potential.append(jnp.sum(acc, axis=0, keepdims=True) + nf[3 * lb + g])
        return field, potential

    def new_state(field, potential):
        mu = [
            [pol[b : b + 1] * (fixed[a : a + 1, lanes(b)] + field[a][b]) for b in range(lb)]
            for a in range(3)
        ]
        q = [base[g : g + 1] - resp[g : g + 1] * potential[g] for g in range(lg)]
        return mu, q

    scope = jax.named_scope
    with scope("send0"):
        share_sums(0)
        share_group(pos, own * prows, prows, S_POS)
        share_state(0)
    for k in range(ITERS):
        with scope(f"share_cell#k={k}"):
            share_cell(k)
        with scope(f"forward#k={k}"):
            if k == 0:
                forward(pos, prows, S_POS, S_PL, S_PR)
            forward(windows[k], urows, S_W + k, S_FL + k, S_FR + k)
        if k == 0:
            with scope("wait_pos"):
                arrived(pos, prows, S_PL, S_PR)
            with scope("build"):
                build()
        with scope(f"wait_window#k={k}"):
            arrived(windows[k], urows, S_FL + k, S_FR + k)
        with scope(f"near#k={k}"):
            apply_near(windows[k])
        with scope(f"wait_far#k={k}"):
            drain(tables[k].at[pl.ds(0, ncell - 1)], recv_sem.at[S_TB + k])
        with scope(f"far#k={k}"):
            field, potential = apply_far(k)
        if k < ITERS - 1:
            with scope(f"put#k={k}"):
                put_state(k + 1, *new_state(field, potential))
            with scope(f"send#k={k + 1}"):
                share_sums(k + 1)
                share_state(k + 1)
        else:
            mu, q = new_state(field, potential)
            for a in range(3):
                for b in range(lb):
                    out_mu[a : a + 1, lanes(b)] = mu[a][b]
            for g in range(lg):
                out_q[g : g + 1] = q[g]

    def sent(ref, rows, sem_group, sem_left, sem_right):
        size = ngrp * rows
        drain(ref.at[pl.ds(0, (ngrp - 1) * rows)], send_sem.at[sem_group])

        @pl.when(cell < ncell - 1)
        def _():
            drain(ref.at[pl.ds(0, size)], send_sem.at[sem_right])

        @pl.when(cell > 0)
        def _():
            drain(ref.at[pl.ds(0, size)], send_sem.at[sem_left])

    sent(pos, prows, S_POS, S_PL, S_PR)
    for k in range(ITERS):
        drain(sa.at[pl.ds(0, ngrp - 1)], send_sem.at[S_SA + k])
        drain(tables[k].at[pl.ds(0, ncell - 1)], send_sem.at[S_TB + k])
        sent(windows[k], urows, S_W + k, S_FL + k, S_FR + k)


def body(
    ncell, ngrp,
    atom_sites, grid_points, dipole_guess, fixed_field, polarisability, base_charge, response,
    near_blocks, grid_blocks, source_blocks,
):
    lb, nb = near_blocks.shape
    nq = grid_blocks.shape[1]
    lg, nm = source_blocks.shape
    urows = 3 * lb + lg
    prows = 3 * lb + 3 * lg
    vmem = pl.BlockSpec(memory_space=pltpu.VMEM)
    tile = (BLOCK, BLOCK)
    window = pltpu.VMEM((3 * ngrp * urows, 1, BLOCK), F32)
    table = pltpu.VMEM((ncell, 1, BLOCK), F32)
    mu, q = pl.pallas_call(
        functools.partial(kernel, ncell, ngrp, lb, lg, nb, nq, nm),
        out_shape=(
            pltpu.VMEM((3, lb * BLOCK), F32),
            pltpu.VMEM((lg, BLOCK), F32),
        ),
        in_specs=[pl.BlockSpec(memory_space=pl.ANY)] * 10,
        out_specs=(vmem, vmem),
        scratch_shapes=[
            pltpu.SMEM(near_blocks.shape, jnp.int32),
            pltpu.SMEM(grid_blocks.shape, jnp.int32),
            pltpu.SMEM(source_blocks.shape, jnp.int32),
            pltpu.VMEM((3, lb * BLOCK), F32),
            pltpu.VMEM((3, lg * BLOCK), F32),
            pltpu.VMEM((3, lb * BLOCK), F32),
            pltpu.VMEM((3, lb * BLOCK), F32),
            pltpu.VMEM((lb, BLOCK), F32),
            pltpu.VMEM((lg, BLOCK), F32),
            pltpu.VMEM((lg, BLOCK), F32),
            pltpu.SMEM((lb * (nb + 1 + nq) + lg * nm,), jnp.int32),
            pltpu.SMEM((lb * (nb + 1 + nq) + lg * nm,), jnp.int32),
            window, window, window,
            pltpu.VMEM((3 * ngrp * prows, 1, BLOCK), F32),
            pltpu.VMEM((ITERS * ngrp, 1, BLOCK), F32),
            table, table, table,
            pltpu.VMEM(((lb + lg) * 3, *tile), F32),
            pltpu.VMEM((lb * (nb + 1) * 4, *tile), F32),
            pltpu.VMEM((lb * nq * 3, *tile), F32),
            pltpu.VMEM((lg * nm * 3, *tile), F32),
            pltpu.VMEM((lb * 9, ncell, BLOCK), F32),
            pltpu.VMEM((lg * 3, ncell, BLOCK), F32),
            pltpu.VMEM((7, ncell, BLOCK), F32),
            pltpu.VMEM(((nb + 1) * 3 + nq, 8, BLOCK), F32),
            pltpu.VMEM((3 * lb + lg, *tile), F32),
            pltpu.VMEM((3 * lb + lg, 1, BLOCK), F32),
            pltpu.SemaphoreType.DMA((10,)),
            pltpu.SemaphoreType.DMA((18,)),
            pltpu.SemaphoreType.DMA((18,)),
        ],
        compiler_params=pltpu.CompilerParams(
            collective_id=0, has_side_effects=True, vmem_limit_bytes=60 * 1024 * 1024
        ),
    )(
        near_blocks, grid_blocks, source_blocks,
        atom_sites, grid_points, dipole_guess, fixed_field,
        polarisability.reshape(lb, BLOCK), base_charge.reshape(lg, BLOCK),
        response.reshape(lg, BLOCK),
    )
    return mu, q.reshape(-1)


def solution(mesh):
    shared = P(None, ("cell", "grp"))
    flat = P(("cell", "grp"))
    rows = P(("cell", "grp"), None)
    return jax.shard_map(
        functools.partial(body, mesh.shape["cell"], mesh.shape["grp"]),
        mesh=mesh,
        in_specs=(shared, shared, shared, shared, flat, flat, flat, rows, rows, rows),
        out_specs=(shared, flat),
        check_vma=False,
    )
```

time: 70.8 us -> 56.7 us (0.80)
  Pallas kernels: 65.5 us -> 54.8 us
  local copies, waits for them, and re-layouts: 3.76 us -> 1.18 us
    pallas_call x1, Pallas kernels: 65.5 us -> 54.8 us  [body(): pl.pallas_call(functools.partial(kernel, ncell, ngrp, lb, lg, nb, nq, nm)...]
    reshape x2 -> x0, local copies, waits for them, and re-layouts: 1.81 us -> none  [the longest x1 1.25 us: body(): base_charge.reshape(1, -1)]
    unnamed x5 -> x2, local copies, waits for them, and re-layouts: 1.95 us -> 1.18 us
where the time goes in v2:
time: 56.7 us; the launch traced here: 56.6 us
  Pallas kernels  54.8 us (97%)
  local copies, waits for them, and re-layouts  1.18 us (2%)
  between operations  0.64 us (1%)
    pallas_call x1, Pallas kernels, body(): pl.pallas_call(functools.partial(kernel, ncell, ngrp, lb, lg, nb, nq, nm)...  54.8 us
    unnamed x2, local copies, waits for them, and re-layouts  1.18 us

profile of v2, /device:TPU:1, one launch (start us, length us, event | category | flops | bytes accessed | tf_op | source)
XLA Modules:
  0.0 56.6 jit_solution(7535573635375059150)
XLA Ops:
  0.6 54.8 %shard_map.113 = (f32[3,512]{1,0:T(4,128)S(1)}, f32[3,128]{1,0:T(4,128)S(1)}) custom-call(s32[4,8]{1,0:T(4,128)} %near_in.1, s32[4,4]{1,0:T(4,128)} %grid_in.1, s32[3,8]{1,0:T(4,128)} %source_in.1, f32[3,512]{1,0:T(4,128)} %sites_in.1, f32[3,384]{1,0:T(4,128)} %points_in.1, f32[3,512]{1,0:T(4,128)} %guess_in.1, f32[3,512]{1,0:T(4,128)} %fixed_in.1, ...), custom_call_target="tpu_custom_call" | custom-call | tf_op jit(solution)/shard_map/pallas_call | solution.py:528
  55.4 0.6 %copy.14 = f32[3,512]{1,0:T(4,128)} copy(f32[3,512]{1,0:T(4,128)S(1)} %get-tuple-element.6) | data formatting | bytes 12288
  56.0 0.6 %copy.15 = f32[384]{0:T(512)} copy(f32[384]{0:T(512)S(1)} %bitcast.4) | data formatting | bytes 3072

commit v3 on v2

--- a/solution.py
+++ b/solution.py
@@ -12,6 +12,8 @@
 CHUNK = 32
 SOFT = 0.04
 ROOT3 = 3.0**0.5
+DIRECT_P = False
+DIRECT_W = (False, True, True)
 MESH = pl.DeviceIdType.MESH
 F32 = jnp.float32
 
@@ -67,8 +69,8 @@
     sites, points, guess, fixed, pol, base, resp,
     urow, prow,
     w0, w1, w2, pos, sa, tb0, tb1, tb2,
-    tgt, td, tc, tp, fd, fp, fb, mub, accs, nf,
-    local_sem, send_sem, recv_sem,
+    tgt, td, tc, tp, fd, fp, zst, lin, lint, tab, mub, accs, nf,
+    local_sem, send_sem, recv_sem, hello,
 ):
     windows = (w0, w1, w2)
     tables = (tb0, tb1, tb2)
@@ -79,6 +81,29 @@
     slots = nb + 1
     own = ngrp + grp
 
+    others = far_order(ncell)
+
+    def cell_at(d):
+        return (cell + d) & (ncell - 1)
+
+    def group_at(d):
+        return (grp + d) & (ngrp - 1)
+
+    def signal(sem, to_cell, to_grp):
+        pl.semaphore_signal(sem, inc=1, device_id=(to_cell, to_grp), device_id_type=MESH)
+
+    beside = cell_at(2 * (cell & 1) - 1)
+    partner = cell ^ 1
+    line = cell & 14
+    z_line = [(cell - line) + ((line + 2 * d) & 14) for d in ring_order(8)]
+    x_line = [cell_at(16 * d) for d in range(1, ncell // 16)]
+    barrier = pltpu.get_barrier_semaphore()
+    with jax.named_scope("greet"):
+        for d in ring_order(ngrp):
+            signal(barrier, cell, group_at(d))
+        for other in z_line + x_line + [beside, partner]:
+            signal(barrier, other, grp)
+    greeted = ngrp - 1 + len(z_line) + len(x_line) + 2
     loads = [
         pltpu.make_async_copy(src, dst, local_sem.at[n])
         for n, (src, dst) in enumerate(
@@ -91,32 +116,30 @@
     ]
     for load in loads:
         load.start()
-    others = far_order(ncell)
-
-    def cell_at(d):
-        return (cell + d) & (ncell - 1)
-
-    def group_at(d):
-        return (grp + d) & (ngrp - 1)
-
-    barrier = pltpu.get_barrier_semaphore()
-    with jax.named_scope("greet"):
-        for d in others:
-            pl.semaphore_signal(
-                barrier, inc=1, device_id=(cell_at(d), grp), device_id_type=MESH
-            )
-        for d in ring_order(ngrp):
-            pl.semaphore_signal(
-                barrier, inc=1, device_id=(cell, group_at(d)), device_id_type=MESH
-            )
     for load in loads:
         load.wait()
 
+    tiles = BLOCK // 8
+
+    def tile(t):
+        return pl.ds(8 * t, 8)
+
     def lanes(j):
         return pl.ds(j * BLOCK, BLOCK)
 
     zc = [cell.astype(F32) + 0.5, 0.5, 0.5]
     lane = lax.broadcasted_iota(jnp.int32, (1, BLOCK), 1)
+
+    def put_sums(k, mu, q):
+        sums = [functools.reduce(jnp.add, mu[a]) for a in range(3)]
+        sums.append(functools.reduce(jnp.add, q))
+        for a in range(3):
+            moment = functools.reduce(jnp.add, [q[g] * offsets(a, g) for g in range(lg)])
+            sums.append(moment + sums[a])
+        row = jnp.zeros((1, BLOCK), F32)
+        for n, total in enumerate(sums):
+            row = jnp.where(lane == n, jnp.sum(total, axis=1, keepdims=True), row)
+        sa[k * ngrp + grp] = row
 
     def put_state(k, mu, q):
         w = windows[k]
@@ -125,28 +148,21 @@
                 w[own * urows + a * lb + b] = mu[a][b]
         for g in range(lg):
             w[own * urows + 3 * lb + g] = q[g]
-        sums = [functools.reduce(jnp.add, mu[a]) for a in range(3)]
-        sums.append(functools.reduce(jnp.add, q))
-        for a in range(3):
-            moment = functools.reduce(
-                jnp.add, [q[g] * (points[a : a + 1, lanes(g)] - zc[a]) for g in range(lg)]
-            )
-            sums.append(moment + sums[a])
-        row = jnp.zeros((1, BLOCK), F32)
-        for n, s in enumerate(sums):
-            row = jnp.where(lane == n, jnp.sum(s, axis=1, keepdims=True), row)
-        sa[k * ngrp + grp] = row
+
+    def offsets(a, g):
+        return points[a : a + 1, lanes(g)] - zc[a]
 
     for a in range(3):
         for b in range(lb):
             pos[own * prows + a * lb + b] = sites[a : a + 1, lanes(b)]
         for g in range(lg):
             pos[own * prows + 3 * lb + a * lg + g] = points[a : a + 1, lanes(g)]
-    put_state(
-        0,
+    first = (
         [[guess[a : a + 1, lanes(b)] for b in range(lb)] for a in range(3)],
         [base[g : g + 1] for g in range(lg)],
     )
+    put_sums(0, *first)
+    put_state(0, *first)
 
     def atom_rows(n, w):
         at, b = lax.shift_right_logical(w, lb.bit_length() - 1), w & (lb - 1)
@@ -186,50 +202,8 @@
     def _():
         clear(2)
 
-    for a in range(3):
-        for b in range(lb):
-            tgt[b * 3 + a] = jnp.transpose(
-                jnp.broadcast_to(sites[a : a + 1, lanes(b)], (BLOCK, BLOCK))
-            )
-        for g in range(lg):
-            tgt[(lb + g) * 3 + a] = jnp.transpose(
-                jnp.broadcast_to(points[a : a + 1, lanes(g)], (BLOCK, BLOCK))
-            )
-
-    cells8 = lax.broadcasted_iota(jnp.int32, (8, BLOCK), 0)
-
-    def far_rows(ref, j, c8):
-        number = cells8 + c8 * 8
-        dx = ref[0:1, lanes(j)] - (number.astype(F32) + 0.5)
-        dy = ref[1:2, lanes(j)] - 0.5 + jnp.zeros_like(dx)
-        dz = ref[2:3, lanes(j)] - 0.5 + jnp.zeros_like(dx)
-        keep = jnp.abs(number - cell) >= 2
-        s1, s3 = powers(dx, dy, dz)
-        s3 = jnp.where(keep, s3, 0.0)
-        return dx, dy, dz, s3, s3 * s1 * s1
-
-    def far_build(c8, carry):
-        row = pl.ds(pl.multiple_of(c8 * 8, 8), 8)
-        for b in range(lb):
-            dx, dy, dz, s3, s5 = far_rows(sites, b, c8)
-            for n, v in enumerate(pair_tensor(dx, dy, dz, s3, s5)):
-                fd[b * 9 + n, row] = v
-            for n, v in enumerate((dx, dy, dz)):
-                fd[b * 9 + 6 + n, row] = v * s3
-        for g in range(lg):
-            dx, dy, dz, s3, s5 = far_rows(points, g, c8)
-            for n, v in enumerate((dx, dy, dz)):
-                fp[g * 3 + n, row] = v * s3
-        return carry
-
-    with jax.named_scope("far_build"):
-        lax.fori_loop(0, ncell // 8, far_build, 0)
-
-    with jax.named_scope("barrier"):
-        pl.semaphore_wait(barrier, ncell + ngrp - 2)
-
     S_SA, S_W, S_FL, S_FR, S_TB = 0, 3, 6, 9, 12
-    S_POS, S_PL, S_PR = 15, 16, 17
+    S_POS, S_PL, S_PR, S_LIN = 15, 16, 17, 18
 
     def share_group(ref, start, count, sem):
         part = ref.at[pl.ds(start, count)]
@@ -239,12 +213,63 @@
     def share_sums(k):
         share_group(sa, k * ngrp + grp, 1, S_SA + k)
 
+    def share_direct(ref, rows, sem_group, sem_left, sem_right):
+        part = ref.at[pl.ds(own * rows, rows)]
+        left = ref.at[pl.ds(grp * rows, rows)]
+        right = ref.at[pl.ds((2 * ngrp + grp) * rows, rows)]
+        for d in ring_order(ngrp):
+            copy_to(
+                part, part, send_sem.at[sem_group], recv_sem.at[sem_group], (cell, group_at(d))
+            )
+
+        beyond = ring_order(ngrp) + [0]
+
+        @pl.when(((cell & 1) == 1) & (cell < ncell - 1))
+        def _():
+            for d in beyond:
+                copy_to(
+                    part, left,
+                    send_sem.at[sem_right], recv_sem.at[sem_right], (cell + 1, group_at(d)),
+                )
+
+        @pl.when(((cell & 1) == 0) & (cell > 0))
+        def _():
+            for d in beyond:
+                copy_to(
+                    part, right,
+                    send_sem.at[sem_left], recv_sem.at[sem_left], (cell - 1, group_at(d)),
+                )
+
+    def forward_partner(ref, rows, sem_group, sem_left, sem_right):
+        drain(ref.at[pl.ds(0, (ngrp - 1) * rows)], recv_sem.at[sem_group])
+        size = ngrp * rows
+        mine = ref.at[pl.ds(size, size)]
+
+        @pl.when((cell & 1) == 0)
+        def _():
+            copy_to(
+                mine, ref.at[pl.ds(0, size)],
+                send_sem.at[sem_right], recv_sem.at[sem_right], (cell + 1, grp),
+            )
+
+        @pl.when((cell & 1) == 1)
+        def _():
+            copy_to(
+                mine, ref.at[pl.ds(2 * size, size)],
+                send_sem.at[sem_left], recv_sem.at[sem_left], (cell - 1, grp),
+            )
+
     def share_state(k):
-        share_group(windows[k], own * urows, urows, S_W + k)
-
-    def share_cell(k):
+        if DIRECT_W[k]:
+            share_direct(windows[k], urows, S_W + k, S_FL + k, S_FR + k)
+        else:
+            share_group(windows[k], own * urows, urows, S_W + k)
+
+    def share_cell(k, answer):
         drain(sa.at[pl.ds(0, ngrp - 1)], recv_sem.at[S_SA + k])
         total = functools.reduce(jnp.add, [sa[k * ngrp + j] for j in range(ngrp)])
+        if answer is not None:
+            total = total + answer
         table = tables[k]
         table[cell] = total
 
@@ -283,11 +308,6 @@
         @pl.when(cell < ncell - 1)
         def _():
             drain(ref.at[pl.ds(2 * size, size)], recv_sem.at[sem_left])
-
-    tiles = BLOCK // 8
-
-    def tile(t):
-        return pl.ds(8 * t, 8)
 
     def wide(row):
         return jnp.broadcast_to(row, (8, BLOCK))
@@ -395,19 +415,17 @@
                 r = urow[A_SRC + g * nm + s]
                 for a in range(3):
                     mub[s * 3 + a] = wide(w[r + a * lb])
-            for c in range(BLOCK // CHUNK):
-                rows = [tile(c * parts + i) for i in range(parts)]
-                acc = [jnp.zeros((8, BLOCK), F32) for _ in range(parts)]
-                for s in range(nm):
-                    m = [mub[s * 3 + a] for a in range(3)]
-                    at = (g * nm + s) * 3
-                    for i in range(parts):
-                        acc[i] = acc[i] + (
-                            tp[at, rows[i]] * m[0] + tp[at + 1, rows[i]] * m[1]
-                            + tp[at + 2, rows[i]] * m[2]
-                        )
-                for i in range(parts):
-                    accs[3 * lb + g, rows[i]] = acc[i]
+            acc = [jnp.zeros((8, BLOCK), F32) for _ in range(tiles)]
+            for s in range(nm):
+                m = [mub[s * 3 + a] for a in range(3)]
+                at = (g * nm + s) * 3
+                for i in range(tiles):
+                    acc[i] = acc[i] + (
+                        tp[at, tile(i)] * m[0] + tp[at + 1, tile(i)] * m[1]
+                        + tp[at + 2, tile(i)] * m[2]
+                    )
+            for i in range(tiles):
+                accs[3 * lb + g, tile(i)] = acc[i]
             reduce_rows(3 * lb - 3 + g)
             return carry
 
@@ -417,33 +435,51 @@
 
     def apply_far(k):
         table = tables[k]
+        acc = [[jnp.zeros((8, BLOCK), F32) for _ in range(lb)] for _ in range(3)]
+        pot = [jnp.zeros((8, BLOCK), F32) for _ in range(lg)]
+        for c in range(ncell):
+            tab[c : c + 1] = table[c]
         for c8 in range(ncell // 8):
-            rows = table[pl.ds(c8 * 8, 8)].reshape(8, BLOCK)
-            for n in range(7):
-                fb[n, pl.ds(c8 * 8, 8)] = jnp.broadcast_to(rows[:, n : n + 1], (8, BLOCK))
-        field = [[None] * lb for _ in range(3)]
-        for b in range(lb):
-            acc = [jnp.zeros((8, BLOCK), F32) for _ in range(3)]
-            for c8 in range(ncell // 8):
-                row = pl.ds(c8 * 8, 8)
+            row = tile(c8)
+            rows = tab[row]
+            px, py, pz, q, mx, my, mz = [
+                jnp.broadcast_to(rows[:, n : n + 1], (8, BLOCK)) for n in range(7)
+            ]
+            for b in range(lb):
                 xx, xy, xz, yy, yz, zz, cx, cy, cz = [fd[b * 9 + n, row] for n in range(9)]
-                q, mx, my, mz = [fb[n, row] for n in range(3, 7)]
-                acc[0] = acc[0] + ((xx * mx + xy * my) + (xz * mz + cx * q))
-                acc[1] = acc[1] + ((xy * mx + yy * my) + (yz * mz + cy * q))
-                acc[2] = acc[2] + ((xz * mx + yz * my) + (zz * mz + cz * q))
-            for a in range(3):
-                field[a][b] = jnp.sum(acc[a], axis=0, keepdims=True) + nf[b * 3 + a]
-        potential = []
-        for g in range(lg):
-            acc = jnp.zeros((8, BLOCK), F32)
-            for c8 in range(ncell // 8):
-                row = pl.ds(c8 * 8, 8)
-                acc = acc + (
-                    fp[g * 3, row] * fb[0, row] + fp[g * 3 + 1, row] * fb[1, row]
-                    + fp[g * 3 + 2, row] * fb[2, row]
+                acc[0][b] = acc[0][b] + ((xx * mx + xy * my) + (xz * mz + cx * q))
+                acc[1][b] = acc[1][b] + ((xy * mx + yy * my) + (yz * mz + cy * q))
+                acc[2][b] = acc[2][b] + ((xz * mx + yz * my) + (zz * mz + cz * q))
+            for g in range(lg):
+                pot[g] = pot[g] + (
+                    fp[g * 3, row] * px + fp[g * 3 + 1, row] * py + fp[g * 3 + 2, row] * pz
                 )
-            potential.append(jnp.sum(acc, axis=0, keepdims=True) + nf[3 * lb + g])
+        field = [
+            [jnp.sum(acc[a][b], axis=0, keepdims=True) + nf[b * 3 + a] for b in range(lb)]
+            for a in range(3)
+        ]
+        potential = [
+            jnp.sum(pot[g], axis=0, keepdims=True) + nf[3 * lb + g] for g in range(lg)
+        ]
         return field, potential
+
+    def far_answer():
+        rows = tab[...]
+        flat = jnp.transpose(jnp.concatenate([rows, rows], axis=0))
+        px, py, pz, q, mx, my, mz = [flat[n : n + 1] for n in range(7)]
+        left = lane < ncell
+        halves = (
+            jnp.where(left, mx, my), jnp.where(left, mz, q),
+            jnp.where(left, px, py), jnp.where(left, pz, 0.0),
+        )
+        total = functools.reduce(jnp.add, [lint[t] * halves[t] for t in range(4)])
+        total = jnp.sum(total, axis=1, keepdims=True)
+        lanes8 = lax.broadcasted_iota(jnp.int32, (8, BLOCK), 1)
+        return jnp.sum(jnp.where(lanes8 == cells8, total, 0.0), axis=0, keepdims=True)
+
+    def near_state():
+        none = [[nf[b * 3 + a] for b in range(lb)] for a in range(3)]
+        return new_state(none, [nf[3 * lb + g] for g in range(lg)])
 
     def new_state(field, potential):
         mu = [
@@ -454,18 +490,104 @@
         return mu, q
 
     scope = jax.named_scope
+    with scope("barrier"):
+        pl.semaphore_wait(barrier, greeted)
+    signal(hello.at[0], beside, grp)
+    for other in z_line:
+        signal(hello.at[1], other, grp)
     with scope("send0"):
         share_sums(0)
-        share_group(pos, own * prows, prows, S_POS)
+        if DIRECT_P:
+            share_direct(pos, prows, S_POS, S_PL, S_PR)
+        else:
+            share_group(pos, own * prows, prows, S_POS)
         share_state(0)
+    for a in range(3):
+        for b in range(lb):
+            tgt[b * 3 + a] = jnp.transpose(
+                jnp.broadcast_to(sites[a : a + 1, lanes(b)], (BLOCK, BLOCK))
+            )
+        for g in range(lg):
+            tgt[(lb + g) * 3 + a] = jnp.transpose(
+                jnp.broadcast_to(points[a : a + 1, lanes(g)], (BLOCK, BLOCK))
+            )
+
+    cells8 = lax.broadcasted_iota(jnp.int32, (8, BLOCK), 0)
+
+    def far_rows(ref, j, c8):
+        number = cells8 + c8 * 8
+        dx = ref[0:1, lanes(j)] - (number.astype(F32) + 0.5)
+        dy = ref[1:2, lanes(j)] - 0.5 + jnp.zeros_like(dx)
+        dz = ref[2:3, lanes(j)] - 0.5 + jnp.zeros_like(dx)
+        keep = jnp.abs(number - cell) >= 2
+        s1, s3 = powers(dx, dy, dz)
+        s3 = jnp.where(keep, s3, 0.0)
+        return dx, dy, dz, s3, s3 * s1 * s1
+
+    def far_build(c8, carry):
+        row = pl.ds(pl.multiple_of(c8 * 8, 8), 8)
+        low = pl.ds(pl.multiple_of(ncell + c8 * 8, 8), 8)
+        answer = [jnp.zeros((8, BLOCK), F32) for _ in range(9)]
+        for b in range(lb):
+            dx, dy, dz, s3, s5 = far_rows(sites, b, c8)
+            values = (*pair_tensor(dx, dy, dz, s3, s5), dx * s3, dy * s3, dz * s3)
+            for n, v in enumerate(values):
+                fd[b * 9 + n, row] = v
+                answer[n] = answer[n] + v * pol[b : b + 1]
+        charge = [[jnp.zeros((8, BLOCK), F32) for _ in range(3)] for _ in range(4)]
+        for g in range(lg):
+            dx, dy, dz, s3, s5 = far_rows(points, g, c8)
+            for n, v in enumerate((dx, dy, dz)):
+                fp[g * 3 + n, row] = v * s3
+                change = v * s3 * resp[g : g + 1]
+                charge[0][n] = charge[0][n] - change
+                for a in range(3):
+                    charge[1 + a][n] = charge[1 + a][n] - change * offsets(a, g)
+        xx, xy, xz, yy, yz, zz, cx, cy, cz = answer
+        halves = [(xx, xy), (xy, yy), (xz, yz), (xz, cx), (yz, cy), (zz, cz)]
+        halves += [(c[0], c[1]) for c in charge]
+        halves += [(c[2], jnp.zeros((8, BLOCK), F32)) for c in charge]
+        for n, (top, bottom) in enumerate(halves):
+            zst[n, row] = top
+            zst[n, low] = bottom
+        return carry
+
+    with jax.named_scope("far_build"):
+        lax.fori_loop(0, ncell // 8, far_build, 0)
+        places = [
+            [(a, a) for a in range(3)] + [(4 + a, a) for a in range(3)],
+            [(a, 3 + a) for a in range(3)] + [(4 + a, 3 + a) for a in range(3)],
+            [(3 + a, 6 + a) for a in range(4)],
+            [(3 + a, 10 + a) for a in range(4)],
+        ]
+        flat = [jnp.sum(jnp.transpose(zst[n]), axis=0, keepdims=True) for n in range(14)]
+        for t in range(4):
+            value = jnp.zeros((8, BLOCK), F32)
+            for at, n in places[t]:
+                value = jnp.where(cells8 == at, flat[n], value)
+            lin[grp, t] = value
+
+    with scope("hello"):
+        pl.semaphore_wait(hello.at[1], len(z_line))
+        signal(hello.at[2], partner, grp)
+        pl.semaphore_wait(hello.at[2], 1)
+        pl.semaphore_wait(hello.at[0], 1)
+    answer = None
     for k in range(ITERS):
         with scope(f"share_cell#k={k}"):
-            share_cell(k)
+            share_cell(k, answer)
         with scope(f"forward#k={k}"):
             if k == 0:
-                forward(pos, prows, S_POS, S_PL, S_PR)
-            forward(windows[k], urows, S_W + k, S_FL + k, S_FR + k)
+                (forward_partner if DIRECT_P else forward)(pos, prows, S_POS, S_PL, S_PR)
+            (forward_partner if DIRECT_W[k] else forward)(
+                windows[k], urows, S_W + k, S_FL + k, S_FR + k
+            )
         if k == 0:
+            for d in ring_order(ngrp):
+                copy_to(
+                    lin.at[grp], lin.at[grp], send_sem.at[S_LIN], recv_sem.at[S_LIN],
+                    (cell, group_at(d)),
+                )
             with scope("wait_pos"):
                 arrived(pos, prows, S_PL, S_PR)
             with scope("build"):
@@ -474,18 +596,26 @@
             arrived(windows[k], urows, S_FL + k, S_FR + k)
         with scope(f"near#k={k}"):
             apply_near(windows[k])
+        if k < ITERS - 1:
+            with scope(f"sums#k={k + 1}"):
+                put_sums(k + 1, *near_state())
+                share_sums(k + 1)
+        if k == 0:
+            with scope("lin"):
+                drain(lin.at[pl.ds(0, ngrp - 1)], recv_sem.at[S_LIN])
+                for t in range(4):
+                    lint[t] = functools.reduce(jnp.add, [lin[j, t] for j in range(ngrp)])
         with scope(f"wait_far#k={k}"):
             drain(tables[k].at[pl.ds(0, ncell - 1)], recv_sem.at[S_TB + k])
         with scope(f"far#k={k}"):
-            field, potential = apply_far(k)
+            mu, q = new_state(*apply_far(k))
         if k < ITERS - 1:
-            with scope(f"put#k={k}"):
-                put_state(k + 1, *new_state(field, potential))
             with scope(f"send#k={k + 1}"):
-                share_sums(k + 1)
+                put_state(k + 1, mu, q)
                 share_state(k + 1)
+            with scope(f"answer#k={k + 1}"):
+                answer = far_answer()
         else:
-            mu, q = new_state(field, potential)
             for a in range(3):
                 for b in range(lb):
                     out_mu[a : a + 1, lanes(b)] = mu[a][b]
@@ -505,6 +635,7 @@
             drain(ref.at[pl.ds(0, size)], send_sem.at[sem_left])
 
     sent(pos, prows, S_POS, S_PL, S_PR)
+    drain(lin.at[pl.ds(0, ngrp - 1)], send_sem.at[S_LIN])
     for k in range(ITERS):
         drain(sa.at[pl.ds(0, ngrp - 1)], send_sem.at[S_SA + k])
         drain(tables[k].at[pl.ds(0, ncell - 1)], send_sem.at[S_TB + k])
@@ -556,13 +687,17 @@
             pltpu.VMEM((lg * nm * 3, *tile), F32),
             pltpu.VMEM((lb * 9, ncell, BLOCK), F32),
             pltpu.VMEM((lg * 3, ncell, BLOCK), F32),
-            pltpu.VMEM((7, ncell, BLOCK), F32),
+            pltpu.VMEM((14, *tile), F32),
+            pltpu.VMEM((ngrp, 4, 8, BLOCK), F32),
+            pltpu.VMEM((4, 8, BLOCK), F32),
+            pltpu.VMEM((ncell, BLOCK), F32),
             pltpu.VMEM(((nb + 1) * 3 + nq, 8, BLOCK), F32),
             pltpu.VMEM((3 * lb + lg, *tile), F32),
             pltpu.VMEM((3 * lb + lg, 1, BLOCK), F32),
             pltpu.SemaphoreType.DMA((10,)),
-            pltpu.SemaphoreType.DMA((18,)),
-            pltpu.SemaphoreType.DMA((18,)),
+            pltpu.SemaphoreType.DMA((19,)),
+            pltpu.SemaphoreType.DMA((19,)),
+            pltpu.SemaphoreType.REGULAR((3,)),
         ],
         compiler_params=pltpu.CompilerParams(
             collective_id=0, has_side_effects=True, vmem_limit_bytes=60 * 1024 * 1024

time: 56.7 us -> 52.3 us (0.922)
  Pallas kernels: 54.8 us -> 50.4 us
    pallas_call x1, Pallas kernels: 54.8 us -> 50.4 us  [body(): pl.pallas_call(functools.partial(kernel, ncell, ngrp, lb, lg, nb, nq, nm)...]
where the time goes in v3:
time: 52.3 us; the launch traced here: 52.2 us
  Pallas kernels  50.4 us (96%)
  local copies, waits for them, and re-layouts  1.18 us (2%)
  between operations  0.64 us (1%)
    pallas_call x1, Pallas kernels, body(): pl.pallas_call(functools.partial(kernel, ncell, ngrp, lb, lg, nb, nq, nm)...  50.4 us
    unnamed x2, local copies, waits for them, and re-layouts  1.18 us

profile of v3, /device:TPU:1, one launch (start us, length us, event | category | flops | bytes accessed | tf_op | source)
XLA Modules:
  0.0 52.2 jit_solution(4153114082625561933)
XLA Ops:
  0.6 50.4 %shard_map.113 = (f32[3,512]{1,0:T(4,128)S(1)}, f32[3,128]{1,0:T(4,128)S(1)}) custom-call(s32[4,8]{1,0:T(4,128)} %near_in.1, s32[4,4]{1,0:T(4,128)} %grid_in.1, s32[3,8]{1,0:T(4,128)} %source_in.1, f32[3,512]{1,0:T(4,128)} %sites_in.1, f32[3,384]{1,0:T(4,128)} %points_in.1, f32[3,512]{1,0:T(4,128)} %guess_in.1, f32[3,512]{1,0:T(4,128)} %fixed_in.1, ...), custom_call_target="tpu_custom_call" | custom-call | tf_op jit(solution)/shard_map/pallas_call | solution.py:659
  51.0 0.6 %copy.14 = f32[3,512]{1,0:T(4,128)} copy(f32[3,512]{1,0:T(4,128)S(1)} %get-tuple-element.6) | data formatting | bytes 12288
  51.6 0.6 %copy.15 = f32[384]{0:T(512)} copy(f32[384]{0:T(512)S(1)} %bitcast.4) | data formatting | bytes 3072

commit v4 on v3

--- a/solution.py
+++ b/solution.py
@@ -12,8 +12,8 @@
 CHUNK = 32
 SOFT = 0.04
 ROOT3 = 3.0**0.5
-DIRECT_P = False
-DIRECT_W = (False, True, True)
+DIRECT_P = True
+DIRECT_W = (True, True, True)
 MESH = pl.DeviceIdType.MESH
 F32 = jnp.float32
 
@@ -222,6 +222,8 @@
                 part, part, send_sem.at[sem_group], recv_sem.at[sem_group], (cell, group_at(d))
             )
 
+        if ref is pos:
+            pl.semaphore_wait(hello.at[0], 1)
         beyond = ring_order(ngrp) + [0]
 
         @pl.when(((cell & 1) == 1) & (cell < ncell - 1))
@@ -330,7 +332,7 @@
                 if own_block:
                     s3 = jnp.where(diagonal == 8 * t, 0.0, s3)
                 for i, v in enumerate((w * dx, w * dy, w * dz, s3)):
-                    td[n * 4 + i, tile(t)] = v
+                    td[(n * tiles + t) * 4 + i] = v
 
         def charge_slot(ref, j, n, at, step):
             r = prow[n]
@@ -339,46 +341,54 @@
                 dx, dy, dz = deltas(j, t, rows)
                 _, s3 = powers(dx, dy, dz)
                 for i, v in enumerate((dx, dy, dz)):
-                    ref[at * 3 + i, tile(t)] = v * s3
+                    ref[(at * tiles + t) * 3 + i] = v * s3
 
         def atoms(b, carry):
             dipole_slot(b, b * slots, True)
 
-            def pair(i, c):
-                dipole_slot(b, b * slots + 1 + 2 * i, False)
-                dipole_slot(b, b * slots + 2 + 2 * i, False)
+            def some(i, c):
+                for e in range(4):
+                    dipole_slot(b, b * slots + 1 + 4 * i + e, False)
                 return c
 
-            lax.fori_loop(0, nb // 2, pair, 0)
-
-            def charge(i, c):
-                for e in range(2):
-                    at = b * nq + 2 * i + e
-                    charge_slot(tc, b, A_GRID + at, at, lg)
-                return c
-
-            lax.fori_loop(0, nq // 2, charge, 0)
+            lax.fori_loop(0, nb // 4, some, 0)
+
+            for s in range(nq):
+                charge_slot(tc, b, A_GRID + b * nq + s, b * nq + s, lg)
             return carry
 
         lax.fori_loop(0, lb, atoms, 0)
+        forward_window(0)
 
         def grids(i, carry):
-            g = i // (nm // 2)
-            for e in range(2):
-                at = 2 * i + e
+            g = i // (nm // 4)
+            for e in range(4):
+                at = 4 * i + e
                 charge_slot(tp, lb + g, A_SRC + at, at, lb)
             return carry
 
-        lax.fori_loop(0, lg * nm // 2, grids, 0)
+        lax.fori_loop(0, lg * nm // 4, grids, 0)
 
     def reduce_rows(j):
         nf[j] = jnp.sum(jnp.transpose(accs[j]), axis=0, keepdims=True)
 
+    def apply_own(w):
+        def atoms(b, carry):
+            m = [wide(w[own * urows + a * lb + b]) for a in range(3)]
+            for t in range(tiles):
+                vx, vy, vz, s3 = [td[(b * slots * tiles + t) * 4 + n] for n in range(4)]
+                p = vx * m[0] + vy * m[1] + vz * m[2]
+                for a, v in enumerate((vx, vy, vz)):
+                    accs[b * 3 + a, tile(t)] = v * p - s3 * m[a]
+            return carry
+
+        lax.fori_loop(0, lb, atoms, 0)
+
     def apply_near(w):
         parts = CHUNK // 8
 
         def atoms(b, carry):
-            for s in range(slots):
+            for s in range(1, slots):
                 r = urow[b * slots + s]
                 for a in range(3):
                     mub[s * 3 + a] = wide(w[r + a * lb])
@@ -387,12 +397,12 @@
             before = jnp.maximum(b - 1, 0)
             for c in range(BLOCK // CHUNK):
                 rows = [tile(c * parts + i) for i in range(parts)]
-                acc = [[jnp.zeros((8, BLOCK), F32) for _ in range(parts)] for _ in range(3)]
-                for s in range(slots):
+                acc = [[accs[b * 3 + a, row] for row in rows] for a in range(3)]
+                for s in range(1, slots):
                     m = [mub[s * 3 + a] for a in range(3)]
-                    at = (b * slots + s) * 4
+                    at = (b * slots + s) * tiles + c * parts
                     for i in range(parts):
-                        vx, vy, vz, s3 = [td[at + n, rows[i]] for n in range(4)]
+                        vx, vy, vz, s3 = [td[(at + i) * 4 + n] for n in range(4)]
                         p = vx * m[0] + vy * m[1] + vz * m[2]
                         for a, v in enumerate((vx, vy, vz)):
                             acc[a][i] = acc[a][i] + (v * p - s3 * m[a])
@@ -400,7 +410,8 @@
                     q = mub[slots * 3 + s]
                     for i in range(parts):
                         for a in range(3):
-                            acc[a][i] = acc[a][i] + tc[(b * nq + s) * 3 + a, rows[i]] * q
+                            at = (b * nq + s) * tiles + c * parts + i
+                            acc[a][i] = acc[a][i] + tc[at * 3 + a] * q
                 for a in range(3):
                     for i in range(parts):
                         accs[b * 3 + a, rows[i]] = acc[a][i]
@@ -418,11 +429,11 @@
             acc = [jnp.zeros((8, BLOCK), F32) for _ in range(tiles)]
             for s in range(nm):
                 m = [mub[s * 3 + a] for a in range(3)]
-                at = (g * nm + s) * 3
+                at = (g * nm + s) * tiles
                 for i in range(tiles):
                     acc[i] = acc[i] + (
-                        tp[at, tile(i)] * m[0] + tp[at + 1, tile(i)] * m[1]
-                        + tp[at + 2, tile(i)] * m[2]
+                        tp[(at + i) * 3] * m[0] + tp[(at + i) * 3 + 1] * m[1]
+                        + tp[(at + i) * 3 + 2] * m[2]
                     )
             for i in range(tiles):
                 accs[3 * lb + g, tile(i)] = acc[i]
@@ -501,7 +512,6 @@
             share_direct(pos, prows, S_POS, S_PL, S_PR)
         else:
             share_group(pos, own * prows, prows, S_POS)
-        share_state(0)
     for a in range(3):
         for b in range(lb):
             tgt[b * 3 + a] = jnp.transpose(
@@ -567,11 +577,36 @@
                 value = jnp.where(cells8 == at, flat[n], value)
             lin[grp, t] = value
 
+    share_state(0)
     with scope("hello"):
         pl.semaphore_wait(hello.at[1], len(z_line))
         signal(hello.at[2], partner, grp)
         pl.semaphore_wait(hello.at[2], 1)
-        pl.semaphore_wait(hello.at[0], 1)
+    def sent(ref, rows, sem_group, sem_left, sem_right):
+        size = ngrp * rows
+        drain(ref.at[pl.ds(0, (ngrp - 1) * rows)], send_sem.at[sem_group])
+
+        @pl.when(cell < ncell - 1)
+        def _():
+            drain(ref.at[pl.ds(0, size)], send_sem.at[sem_right])
+
+        @pl.when(cell > 0)
+        def _():
+            drain(ref.at[pl.ds(0, size)], send_sem.at[sem_left])
+
+    def sent_all(k):
+        if k == 0:
+            sent(pos, prows, S_POS, S_PL, S_PR)
+            drain(lin.at[pl.ds(0, ngrp - 1)], send_sem.at[S_LIN])
+        drain(sa.at[pl.ds(0, ngrp - 1)], send_sem.at[S_SA + k])
+        drain(tables[k].at[pl.ds(0, ncell - 1)], send_sem.at[S_TB + k])
+        sent(windows[k], urows, S_W + k, S_FL + k, S_FR + k)
+
+    def forward_window(k):
+        (forward_partner if DIRECT_W[k] else forward)(
+            windows[k], urows, S_W + k, S_FL + k, S_FR + k
+        )
+
     answer = None
     for k in range(ITERS):
         with scope(f"share_cell#k={k}"):
@@ -579,9 +614,9 @@
         with scope(f"forward#k={k}"):
             if k == 0:
                 (forward_partner if DIRECT_P else forward)(pos, prows, S_POS, S_PL, S_PR)
-            (forward_partner if DIRECT_W[k] else forward)(
-                windows[k], urows, S_W + k, S_FL + k, S_FR + k
-            )
+            if k > 0:
+                forward_window(k)
+                sent_all(k - 1)
         if k == 0:
             for d in ring_order(ngrp):
                 copy_to(
@@ -592,6 +627,8 @@
                 arrived(pos, prows, S_PL, S_PR)
             with scope("build"):
                 build()
+        with scope(f"own#k={k}"):
+            apply_own(windows[k])
         with scope(f"wait_window#k={k}"):
             arrived(windows[k], urows, S_FL + k, S_FR + k)
         with scope(f"near#k={k}"):
@@ -622,24 +659,7 @@
             for g in range(lg):
                 out_q[g : g + 1] = q[g]
 
-    def sent(ref, rows, sem_group, sem_left, sem_right):
-        size = ngrp * rows
-        drain(ref.at[pl.ds(0, (ngrp - 1) * rows)], send_sem.at[sem_group])
-
-        @pl.when(cell < ncell - 1)
-        def _():
-            drain(ref.at[pl.ds(0, size)], send_sem.at[sem_right])
-
-        @pl.when(cell > 0)
-        def _():
-            drain(ref.at[pl.ds(0, size)], send_sem.at[sem_left])
-
-    sent(pos, prows, S_POS, S_PL, S_PR)
-    drain(lin.at[pl.ds(0, ngrp - 1)], send_sem.at[S_LIN])
-    for k in range(ITERS):
-        drain(sa.at[pl.ds(0, ngrp - 1)], send_sem.at[S_SA + k])
-        drain(tables[k].at[pl.ds(0, ncell - 1)], send_sem.at[S_TB + k])
-        sent(windows[k], urows, S_W + k, S_FL + k, S_FR + k)
+    sent_all(ITERS - 1)
 
 
 def body(
@@ -682,9 +702,9 @@
             pltpu.VMEM((ITERS * ngrp, 1, BLOCK), F32),
             table, table, table,
             pltpu.VMEM(((lb + lg) * 3, *tile), F32),
-            pltpu.VMEM((lb * (nb + 1) * 4, *tile), F32),
-            pltpu.VMEM((lb * nq * 3, *tile), F32),
-            pltpu.VMEM((lg * nm * 3, *tile), F32),
+            pltpu.VMEM((lb * (nb + 1) * 64, 8, BLOCK), F32),
+            pltpu.VMEM((lb * nq * 48, 8, BLOCK), F32),
+            pltpu.VMEM((lg * nm * 48, 8, BLOCK), F32),
             pltpu.VMEM((lb * 9, ncell, BLOCK), F32),
             pltpu.VMEM((lg * 3, ncell, BLOCK), F32),
             pltpu.VMEM((14, *tile), F32),

time: 52.3 us -> 50.6 us (0.967)
  Pallas kernels: 50.4 us -> 48.6 us
    pallas_call x1, Pallas kernels: 50.4 us -> 48.6 us  [body(): pl.pallas_call(functools.partial(kernel, ncell, ngrp, lb, lg, nb, nq, nm)...]
where the time goes in v4:
time: 50.6 us; the launch traced here: 50.4 us
  Pallas kernels  48.6 us (96%)
  local copies, waits for them, and re-layouts  1.18 us (2%)
  between operations  0.64 us (1%)
    pallas_call x1, Pallas kernels, body(): pl.pallas_call(functools.partial(kernel, ncell, ngrp, lb, lg, nb, nq, nm)...  48.6 us
    unnamed x2, local copies, waits for them, and re-layouts  1.18 us

profile of v4, /device:TPU:1, one launch (start us, length us, event | category | flops | bytes accessed | tf_op | source)
XLA Modules:
  0.0 50.4 jit_solution(8995649809959887032)
XLA Ops:
  0.6 48.6 %shard_map.113 = (f32[3,512]{1,0:T(4,128)S(1)}, f32[3,128]{1,0:T(4,128)S(1)}) custom-call(s32[4,8]{1,0:T(4,128)} %near_in.1, s32[4,4]{1,0:T(4,128)} %grid_in.1, s32[3,8]{1,0:T(4,128)} %source_in.1, f32[3,512]{1,0:T(4,128)} %sites_in.1, f32[3,384]{1,0:T(4,128)} %points_in.1, f32[3,512]{1,0:T(4,128)} %guess_in.1, f32[3,512]{1,0:T(4,128)} %fixed_in.1, ...), custom_call_target="tpu_custom_call" | custom-call | tf_op jit(solution)/shard_map/pallas_call | solution.py:679
  49.2 0.6 %copy.14 = f32[3,512]{1,0:T(4,128)} copy(f32[3,512]{1,0:T(4,128)S(1)} %get-tuple-element.6) | data formatting | bytes 12288
  49.8 0.6 %copy.15 = f32[384]{0:T(512)} copy(f32[384]{0:T(512)S(1)} %bitcast.4) | data formatting | bytes 3072

commit v5 on v4

--- a/solution.py
+++ b/solution.py
@@ -69,7 +69,7 @@
     sites, points, guess, fixed, pol, base, resp,
     urow, prow,
     w0, w1, w2, pos, sa, tb0, tb1, tb2,
-    tgt, td, tc, tp, fd, fp, zst, lin, lint, tab, mub, accs, nf,
+    tgt, td, tc, tp, fd, fp, zst, lin, lint, tab, mus, mub, accs, nf,
     local_sem, send_sem, recv_sem, hello,
 ):
     windows = (w0, w1, w2)
@@ -386,6 +386,28 @@
 
     def apply_near(w):
         parts = CHUNK // 8
+
+        def pick_grids(n, carry):
+            r = urow[A_SRC + n]
+            for a in range(3):
+                mus[n * 3 + a] = wide(w[r + a * lb])
+            return carry
+
+        lax.fori_loop(0, lg * nm, pick_grids, 0, unroll=True)
+
+        def grid_part(g, c):
+            acc = [jnp.zeros((8, BLOCK), F32) for _ in range(parts)]
+            for s in range(nm):
+                m = [mus[(g * nm + s) * 3 + a] for a in range(3)]
+                at = (g * nm + s) * tiles + c * parts
+                for i in range(parts):
+                    acc[i] = acc[i] + (
+                        tp[(at + i) * 3] * m[0] + tp[(at + i) * 3 + 1] * m[1]
+                        + tp[(at + i) * 3 + 2] * m[2]
+                    )
+            for i in range(parts):
+                row = pl.ds(pl.multiple_of(c * CHUNK + 8 * i, 8), 8)
+                accs[3 * lb + g, row] = acc[i]
 
         def atoms(b, carry):
             for s in range(1, slots):
@@ -417,30 +439,14 @@
                         accs[b * 3 + a, rows[i]] = acc[a][i]
                 if c < 3:
                     reduce_rows(before * 3 + c)
+                if c < lg:
+                    grid_part(c, b)
             return carry
 
         lax.fori_loop(0, lb, atoms, 0)
 
-        def grids(g, carry):
-            for s in range(nm):
-                r = urow[A_SRC + g * nm + s]
-                for a in range(3):
-                    mub[s * 3 + a] = wide(w[r + a * lb])
-            acc = [jnp.zeros((8, BLOCK), F32) for _ in range(tiles)]
-            for s in range(nm):
-                m = [mub[s * 3 + a] for a in range(3)]
-                at = (g * nm + s) * tiles
-                for i in range(tiles):
-                    acc[i] = acc[i] + (
-                        tp[(at + i) * 3] * m[0] + tp[(at + i) * 3 + 1] * m[1]
-                        + tp[(at + i) * 3 + 2] * m[2]
-                    )
-            for i in range(tiles):
-                accs[3 * lb + g, tile(i)] = acc[i]
-            reduce_rows(3 * lb - 3 + g)
-            return carry
-
-        lax.fori_loop(0, lg, grids, 0)
+        for n in range(3):
+            reduce_rows(3 * (lb - 1) + n)
         for g in range(lg):
             reduce_rows(3 * lb + g)
 
@@ -711,6 +717,7 @@
             pltpu.VMEM((ngrp, 4, 8, BLOCK), F32),
             pltpu.VMEM((4, 8, BLOCK), F32),
             pltpu.VMEM((ncell, BLOCK), F32),
+            pltpu.VMEM((lg * nm * 3, 8, BLOCK), F32),
             pltpu.VMEM(((nb + 1) * 3 + nq, 8, BLOCK), F32),
             pltpu.VMEM((3 * lb + lg, *tile), F32),
             pltpu.VMEM((3 * lb + lg, 1, BLOCK), F32),

time: 50.6 us -> 50.3 us (level)
  no operation moved by 1% of the time
where the time goes in v5:
time: 50.3 us; the launch traced here: 50.1 us
  Pallas kernels  48.3 us (96%)
  local copies, waits for them, and re-layouts  1.18 us (2%)
  between operations  0.64 us (1%)
    pallas_call x1, Pallas kernels, body(): pl.pallas_call(functools.partial(kernel, ncell, ngrp, lb, lg, nb, nq, nm)...  48.3 us
    unnamed x2, local copies, waits for them, and re-layouts  1.18 us

profile of v5, /device:TPU:1, one launch (start us, length us, event | category | flops | bytes accessed | tf_op | source)
XLA Modules:
  0.0 50.1 jit_solution(14732349095581943415)
XLA Ops:
  0.6 48.3 %shard_map.113 = (f32[3,512]{1,0:T(4,128)S(1)}, f32[3,128]{1,0:T(4,128)S(1)}) custom-call(s32[4,8]{1,0:T(4,128)} %near_in.1, s32[4,4]{1,0:T(4,128)} %grid_in.1, s32[3,8]{1,0:T(4,128)} %source_in.1, f32[3,512]{1,0:T(4,128)} %sites_in.1, f32[3,384]{1,0:T(4,128)} %points_in.1, f32[3,512]{1,0:T(4,128)} %guess_in.1, f32[3,512]{1,0:T(4,128)} %fixed_in.1, ...), custom_call_target="tpu_custom_call" | custom-call | tf_op jit(solution)/shard_map/pallas_call | solution.py:685
  48.9 0.6 %copy.14 = f32[3,512]{1,0:T(4,128)} copy(f32[3,512]{1,0:T(4,128)S(1)} %get-tuple-element.6) | data formatting | bytes 12288
  49.5 0.6 %copy.15 = f32[384]{0:T(512)} copy(f32[384]{0:T(512)S(1)} %bitcast.4) | data formatting | bytes 3072
